TPU v7x, 256 devices: a whole 4x4x8 slice. The times are simulated.
256 devices in a mesh: seq: 64 (over z, y, core), head: 4 (over x).
Axes of the slice: x: 4, y: 4, z: 8, core: 2. Of those that a mesh axis runs over, the one named last changes fastest.
Arguments:
- queries: bfloat16 [32768, 8192], P(('seq', 'head')), may hold values from -8 to 8
- keys: bfloat16 [32768, 1024], P(('seq', 'head')), may hold values from -8 to 8
- values: bfloat16 [32768, 1024], P(('seq', 'head')), may hold values from -6 to 6
- selected: int32 [256, 8], P('seq'), may hold values from 0 to 255, as said below
- counts: int32 [256], P('seq'), may hold values from 1 to 8
- block_slot: int32 [256], P('seq'), may hold values from 0 to 255, as said below
Outputs:
- attended: bfloat16 [32768, 8192], P(('seq', 'head'))
Inputs may be any that keep to these rules, and one draw needn't show every extreme that they name: A permutation of 0 to 255. Block b's rows of keys and values start at row 128 * block_slot[b]; its owner shard is block_slot[b] // 4. The 4 blocks of one sequence shard (blocks s * 4 onward) have distinct owner shards, and block_slot[b] % 4 == b % 4. `selected`: row q lists its live entries first: entry 0 is q itself, the other live entries are distinct blocks of earlier sequence shards; entries from counts[q] on are 0. Over the live entries of the 4 rows of one sequence shard, at most 2 distinct blocks have the same owner shard, and in every draw some shard reaches 2 from some owner.
All inputs are finite; a program needn't handle non-finite values.
Results may differ from a plain program's by a relative error of at most 0.0049.
Values may be sent and summed in bfloat16 or wider, within the bound.
A program may use at most 128 MiB of HBM per device.

v0:
```python
import math

import jax
import jax.numpy as jnp
from jax import lax
from jax.sharding import PartitionSpec as P

QUERY_HEADS = 64
KEY_VALUE_HEADS = 8
HEAD_SIZE = 128
BLOCK_ROWS = 128
SELECTION_COUNT = 8
CAP = 2


def laid_out(blocks, dim):
    blocks = jnp.moveaxis(blocks, 0, dim)
    lengths = blocks.shape
    return blocks.reshape(*lengths[:dim], lengths[dim] * lengths[dim + 1], *lengths[dim + 2 :])


def copy_for_each(array, axis):
    count = lax.axis_size(axis)
    return lax.all_to_all(
        jnp.broadcast_to(array[None], (count, *array.shape)), axis, 0, 0, tiled=True
    )


def collect(array, axis, dim):
    return laid_out(copy_for_each(array, axis), dim)


def in_one_piece(arrays, axis, dim, along):
    columns = [a.reshape(*a.shape[:along], -1) for a in arrays]
    both = jnp.concatenate(columns, axis=along)
    out, at, gathered = (collect(both, axis, dim), 0, [])
    for a, column in zip(arrays, columns):
        piece = out[..., at : at + column.shape[along]]
        gathered.append(piece.reshape(*piece.shape[:along], *a.shape[along:]))
        at += column.shape[along]
    return tuple(gathered)


def in_one_piece_2(arrays, axis, split_dim, concat_dim, along):
    both = jnp.concatenate(arrays, axis=along)
    out, at, gathered = (
        lax.all_to_all(both, axis, split_axis=split_dim, concat_axis=concat_dim, tiled=True),
        0,
        [],
    )
    for a in arrays:
        gathered.append(lax.slice_in_dim(out, at, at + a.shape[along], axis=along))
        at += a.shape[along]
    return tuple(gathered)


def body(queries, keys, values, selected, counts, block_slot):
    seq_count = lax.axis_size("seq")
    my_shard = lax.axis_index("seq")
    blk_seq = selected.shape[0]
    block_count = blk_seq * seq_count
    highest = lax.Precision.HIGHEST
    q_heads, k_heads, v_heads = (
        lax.all_to_all(queries, "head", split_axis=1, concat_axis=0, tiled=True),
        lax.all_to_all(keys, "head", split_axis=1, concat_axis=0, tiled=True),
        lax.all_to_all(values, "head", split_axis=1, concat_axis=0, tiled=True),
    )
    kv_width = k_heads.shape[1]
    kv_heads_dev = kv_width // HEAD_SIZE
    all_sel, all_counts, all_slots = in_one_piece((selected, counts, block_slot), "seq", 0, 1)
    block_ids = jnp.arange(block_count, dtype=jnp.int32)
    slot_hit = (all_slots[:, None] == block_ids[None, :]).astype(jnp.float32)
    entry_range = jnp.arange(SELECTION_COUNT, dtype=jnp.int32)
    entry_live = (entry_range[None, :] < counts[:, None]).astype(jnp.float32)
    entry_hit = (selected.reshape(-1)[:, None] == block_ids[None, :]).astype(jnp.float32)
    wanted_blocks = jnp.max(entry_hit * entry_live.reshape(-1, 1), axis=0)
    wanted_slots = jnp.dot(wanted_blocks, slot_hit, precision=highest)
    wanted_grid = wanted_slots.reshape(seq_count, blk_seq)
    rank_grid = jnp.cumsum(wanted_grid, axis=1) - wanted_grid
    owner_base = (jnp.arange(seq_count, dtype=jnp.int32) * CAP).astype(jnp.float32)
    place_slot = (owner_base[:, None] + rank_grid).reshape(-1)
    place_block = jnp.dot(slot_hit, place_slot, precision=highest)
    place_entry = jnp.dot(entry_hit, place_block, precision=highest).astype(jnp.int32)
    place_entry = jnp.clip(place_entry, 0, seq_count * CAP - 1).reshape(blk_seq, SELECTION_COUNT)
    mine_hit = lax.dynamic_slice_in_dim(slot_hit, my_shard * blk_seq, blk_seq, 1)
    mine_ids = jnp.dot(block_ids.astype(jnp.float32), mine_hit, precision=highest).astype(jnp.int32)
    live_all = entry_range[None, :] < all_counts[:, None]
    asked = (all_sel[:, :, None] == mine_ids[None, None, :]) & live_all[:, :, None]
    wanted_by = jnp.max(
        asked.reshape(seq_count, blk_seq * SELECTION_COUNT, blk_seq).astype(jnp.int32), axis=1
    )
    wanted_float = wanted_by.astype(jnp.float32)
    send_rank = jnp.cumsum(wanted_float, axis=1) - wanted_float
    cap_range = jnp.arange(CAP, dtype=jnp.float32)
    pick_map = wanted_float[:, None, :] * (
        send_rank[:, None, :] == cap_range[None, :, None]
    ).astype(jnp.float32)
    pick_map = pick_map.reshape(seq_count * CAP, blk_seq)
    source_tile = jnp.sum(
        pick_map * jnp.arange(blk_seq, dtype=jnp.float32)[None, :], axis=1
    ).astype(jnp.int32)
    is_valid = jnp.sum(pick_map, axis=1) > 0.5
    own_keys = k_heads.reshape(blk_seq, BLOCK_ROWS, kv_width)
    own_values = v_heads.reshape(blk_seq, BLOCK_ROWS, kv_width)
    send_keys = jnp.where(
        is_valid[:, None, None], own_keys[source_tile], jnp.zeros((), jnp.bfloat16)
    )
    send_values = jnp.where(
        is_valid[:, None, None], own_values[source_tile], jnp.zeros((), jnp.bfloat16)
    )
    got_keys, got_values = in_one_piece_2((send_keys, send_values), "seq", 0, 0, 1)
    heads_per_group = QUERY_HEADS // KEY_VALUE_HEADS
    score_scale = 1.0 / math.sqrt(HEAD_SIZE)
    query_block_list = q_heads.reshape(
        blk_seq, BLOCK_ROWS, kv_heads_dev, heads_per_group, HEAD_SIZE
    )
    got_keys = got_keys.reshape(seq_count * CAP, BLOCK_ROWS, kv_heads_dev, HEAD_SIZE)
    got_values = got_values.reshape(seq_count * CAP, BLOCK_ROWS, kv_heads_dev, HEAD_SIZE)
    row_range = jnp.arange(BLOCK_ROWS, dtype=jnp.int32)

    def attend(operands):
        local_block, query_tile, place_row, chosen, live_count = operands
        key_block_rows = got_keys[place_row].reshape(
            SELECTION_COUNT * BLOCK_ROWS, kv_heads_dev, HEAD_SIZE
        )
        value_block_rows = got_values[place_row].reshape(
            SELECTION_COUNT * BLOCK_ROWS, kv_heads_dev, HEAD_SIZE
        )
        scores = (
            jnp.einsum(
                "igmd,kgd->gmik", query_tile, key_block_rows, preferred_element_type=jnp.float32
            )
            * score_scale
        )
        query_pos = (my_shard * blk_seq + local_block) * BLOCK_ROWS + row_range
        key_pos = (chosen[:, None] * BLOCK_ROWS + row_range[None, :]).reshape(-1)
        live_entry = jnp.repeat(entry_range < live_count, BLOCK_ROWS)
        visible = live_entry[None, :] & (key_pos[None, :] <= query_pos[:, None])
        scores = jnp.where(visible[None, None], scores, -jnp.inf)
        row_top = jnp.max(scores, axis=-1, keepdims=True)
        weights = jnp.exp(scores - row_top)
        probability = (weights / jnp.sum(weights, axis=-1, keepdims=True)).astype(jnp.bfloat16)
        mixed_out = jnp.einsum(
            "gmik,kgd->igmd", probability, value_block_rows, preferred_element_type=jnp.float32
        )
        return mixed_out.astype(jnp.bfloat16).reshape(
            BLOCK_ROWS, kv_heads_dev * heads_per_group * HEAD_SIZE
        )

    attended = lax.map(
        attend,
        (jnp.arange(blk_seq, dtype=jnp.int32), query_block_list, place_entry, selected, counts),
    )
    attended = attended.reshape(blk_seq * BLOCK_ROWS, kv_heads_dev * heads_per_group * HEAD_SIZE)
    return lax.all_to_all(attended, "head", split_axis=0, concat_axis=1, tiled=True)


def solution(mesh):
    return jax.shard_map(
        body,
        mesh=mesh,
        in_specs=(
            P(("seq", "head"), None),
            P(("seq", "head"), None),
            P(("seq", "head"), None),
            P("seq", None),
            P("seq"),
            P("seq"),
        ),
        out_specs=P(("seq", "head"), None),
        check_vma=False,
    )
```

profile of v0, /device:TPU:1, one launch (start us, length us, event | category | flops | bytes accessed | tf_op | source)
XLA Modules:
  0.0 603.7 jit_solution(15070980725650697883)
XLA Ops:
  2.9 13.1 %all-to-all-start = ((s32[64,4,10]{2,1,0:T(4,128)}), s32[64,4,10]{2,1,0:T(4,128)S(1)}, u32[]{:S(2)}, u32[]{:S(2)}) async-start(s32[64,4,10]{2,1,0:T(4,128)} %broadcast_in_dim.47), calls=%async_computation | async-start | bytes 262144 | tf_op jit(solution)/shard_map/all_to_all | solution.py:24
  20.1 7.0 %all-to-all-done = s32[64,4,10]{2,1,0:T(4,128)S(1)} async-done(((s32[64,4,10]{2,1,0:T(4,128)}), s32[64,4,10]{2,1,0:T(4,128)S(1)}, u32[]{:S(2)}, u32[]{:S(2)}) %all-to-all-start) | async-done | bytes 10272 | tf_op jit(solution)/shard_map/all_to_all | solution.py:24
  27.1 4.0 all-to-all-start.1
  32.7 4.3 all-to-all-done.1
  40.7 6.3 %gather_fusion.2 = bf16[128,128,256]{2,1,0:T(8,128)(2,1)} fusion(bf16[4,128,256]{2,1,0:T(8,128)(2,1)S(1)} %bitcast.114, s32[1024]{0:T(1024)S(1)} %pad_clamp_fusion.1), kind=kCustom, calls=%fused_computation.2 | custom fusion | bytes 16777728 | tf_op jit(solution)/shard_map/gather | solution.py:106
  47.0 6.3 %gather_fusion.3 = bf16[128,128,256]{2,1,0:T(8,128)(2,1)} fusion(bf16[4,128,256]{2,1,0:T(8,128)(2,1)S(1)} %bitcast.115, s32[1024]{0:T(1024)S(1)} %pad_clamp_fusion.1), kind=kCustom, calls=%fused_computation.3 | custom fusion | bytes 16777728 | tf_op jit(solution)/shard_map/gather | solution.py:109
  53.3 6.7 %broadcast_select_fusion.1 = (bf16[128,128,256]{2,1,0:T(8,128)(2,1)S(1)}, bf16[128,128,256]{2,1,0:T(8,128)(2,1)S(1)}) fusion(bf16[128,128,256]{2,1,0:T(8,128)(2,1)} %gather_fusion.2, pred[128]{0:T(512)(128)(4,1)S(1)} %gt.15, bf16[128,128,256]{2,1,0:T(8,128)(2,1)} %gather_fusion.3), kind=kLoop, calls=%fused_computation.46 | loop fusion | flops 8388608 | bytes 33554560 | tf_op jit(solution)/shard_map/jit(_where)/select_n | solution.py:105
  60.0 6.8 %pad_maximum_fusion = bf16[128,256,256]{2,1,0:T(8,128)(2,1)} fusion(bf16[128,128,256]{2,1,0:T(8,128)(2,1)S(1)} %get-tuple-element.257, bf16[128,128,256]{2,1,0:T(8,128)(2,1)S(1)} %get-tuple-element.256), kind=kLoop, calls=%fused_computation.44 | loop fusion | flops 33554432 | bytes 33554432 | tf_op jit(solution)/shard_map/concatenate | solution.py:45
  66.7 7.2 %all-to-all-start.3 = ((bf16[128,256,256]{2,1,0:T(8,128)(2,1)}), bf16[128,256,256]{2,1,0:T(8,128)(2,1)}, u32[]{:S(2)}, u32[]{:S(2)}) async-start(bf16[128,256,256]{2,1,0:T(8,128)(2,1)} %pad_maximum_fusion), calls=%async_computation.3 | async-start | bytes 33554432 | tf_op jit(solution)/shard_map/all_to_all | solution.py:47
  78.0 362.5 %all-to-all-done.3 = bf16[128,256,256]{2,1,0:T(8,128)(2,1)} async-done(((bf16[128,256,256]{2,1,0:T(8,128)(2,1)}), bf16[128,256,256]{2,1,0:T(8,128)(2,1)}, u32[]{:S(2)}, u32[]{:S(2)}) %all-to-all-start.3) | async-done | bytes 16777248 | tf_op jit(solution)/shard_map/all_to_all | solution.py:47
  440.4 4.5 all-to-all-start.4
  445.2 11.7 %fusion.59 = (bf16[128,128,256]{2,1,0:T(8,128)(2,1)}, bf16[128,128,256]{2,1,0:T(8,128)(2,1)}) fusion(bf16[128,256,256]{2,1,0:T(8,128)(2,1)} %all-to-all-done.3), kind=kLoop, calls=%fused_computation.82 | loop fusion | bytes 33554432 | tf_op jit(solution)/shard_map/slice | solution.py:52
  456.9 12.5 %reshape.311 = bf16[128,128,2,128]{3,2,1,0:T(2,128)(2,1)} reshape(bf16[128,128,256]{2,1,0:T(8,128)(2,1)} %get-tuple-element.255) | data formatting | bytes 16777216 | tf_op jit(solution)/shard_map/reshape | solution.py:118
  469.4 12.5 %reshape.312 = bf16[128,128,2,128]{3,2,1,0:T(2,128)(2,1)} reshape(bf16[128,128,256]{2,1,0:T(8,128)(2,1)} %get-tuple-element.254) | data formatting | bytes 16777216 | tf_op jit(solution)/shard_map/reshape | solution.py:117
  482.0 90.4 %while.14 = (s32[]{:T(128)}, bf16[4,128,2048]{1,2,0:T(8,128)(2,1)}, s32[4,8]{1,0:T(4,128)S(1)}, bf16[128,128,2,128]{3,2,1,0:T(2,128)(2,1)}, s32[4]{0:T(128)S(1)}...) while((s32[]{:T(128)}, bf16[4,128,2048]{1,2,0:T(8,128)(2,1)}, ...), condition=%wide.region_9.10_spmd.clone.clone, body=%wide.region_6.9_spmd.clone.clone.sunk | while | flops 1086852352 | bytes 22314952 | solution.py:150
  484.8 5.0 gather_fusion
  489.8 4.7 fusion.78
  494.5 5.0 gather_fusion.1
  499.5 4.2 fusion.79
  507.4 5.0 gather_fusion
  512.4 4.7 fusion.78
  517.1 5.0 gather_fusion.1
  522.1 4.2 fusion.79
  530.0 5.0 gather_fusion
  535.0 4.7 fusion.78
  539.7 5.0 gather_fusion.1
  544.7 4.2 fusion.79
  552.6 5.0 gather_fusion
  557.6 4.7 fusion.78
  562.3 5.0 gather_fusion.1
  567.3 4.2 fusion.79
  572.4 28.4 %all_to_all.74 = bf16[4,128,2048]{1,2,0:T(8,128)(2,1)S(1)} all-to-all(bf16[4,128,2048]{1,2,0:T(8,128)(2,1)} %get-tuple-element.146), channel_id=1, replica_groups=mesh['seq'=64,'head'=4] {'head'}, dimensions={0} | all-to-all | bytes 4194304 | tf_op jit(solution)/shard_map/all_to_all | solution.py:155
  (105 shorter events, 31.4 us)
Async XLA Ops:
  2.9 24.2 %all-to-all-start = ((s32[64,4,10]{2,1,0:T(4,128)}), s32[64,4,10]{2,1,0:T(4,128)S(1)}, u32[]{:S(2)}, u32[]{:S(2)}) async-start(s32[64,4,10]{2,1,0:T(4,128)} %broadcast_in_dim.47), calls=%async_computation | async-start | bytes 262144 | tf_op jit(solution)/shard_map/all_to_all | solution.py:24
  27.1 9.8 %all-to-all-start.1 = ((bf16[128,4,256]{2,0,1:T(8,128)(2,1)}), bf16[128,4,256]{2,0,1:T(8,128)(2,1)S(1)}, u32[]{:S(2)}, u32[]{:S(2)}) async-start(bf16[128,4,256]{2,0,1:T(8,128)(2,1)} %copy.48), calls=%async_computation.1 | async-start | bytes 524288 | tf_op jit(solution)/shard_map/all_to_all | solution.py:65
  37.0 10.0 %all-to-all-start.2 = ((bf16[128,4,256]{2,0,1:T(8,128)(2,1)}), bf16[128,4,256]{2,0,1:T(8,128)(2,1)S(1)}, u32[]{:S(2)}, u32[]{:S(2)}) async-start(bf16[128,4,256]{2,0,1:T(8,128)(2,1)} %copy.51), calls=%async_computation.2 | async-start | bytes 524288 | tf_op jit(solution)/shard_map/all_to_all | solution.py:66
  66.7 7.3 %copy-start.1 = (s32[4,8]{1,0:T(4,128)S(1)}, s32[4,8]{1,0:T(4,128)}, u32[]{:S(2)}) copy-start(s32[4,8]{1,0:T(4,128)} %param.11) | copy-start | bytes 388
  66.7 7.3 %copy-start.2 = (s32[4]{0:T(128)S(1)}, s32[4]{0:T(128)}, u32[]{:S(2)}) copy-start(s32[4]{0:T(128)} %param.12) | copy-start | bytes 52
  66.7 7.5 %copy-start = (bf16[128,8192]{1,0:T(8,128)(2,1)S(1)}, bf16[128,8192]{1,0:T(8,128)(2,1)}, u32[]{:S(2)}) copy-start(bf16[128,8192]{1,0:T(8,128)(2,1)} %param.8) | copy-start | bytes 6291460
  66.7 373.7 %all-to-all-start.3 = ((bf16[128,256,256]{2,1,0:T(8,128)(2,1)}), bf16[128,256,256]{2,1,0:T(8,128)(2,1)}, u32[]{:S(2)}, u32[]{:S(2)}) async-start(bf16[128,256,256]{2,1,0:T(8,128)(2,1)} %pad_maximum_fusion), calls=%async_computation.3 | async-start | bytes 33554432 | tf_op jit(solution)/shard_map/all_to_all | solution.py:47
  440.4 41.5 %all-to-all-start.4 = ((bf16[128,4,2048]{0,2,1:T(8,128)(2,1)}), bf16[128,4,2048]{0,2,1:T(8,128)(2,1)S(1)}, u32[]{:S(2)}, u32[]{:S(2)}) async-start(bf16[128,4,2048]{0,2,1:T(8,128)(2,1)} %bitcast.16), calls=%async_computation.4 | async-start | bytes 4194304 | tf_op jit(solution)/shard_map/all_to_all | solution.py:64
where the time goes:
time: 613 us; the launch traced here: 604 us
  waiting for transfers between devices  374 us (61%)
  local copies, waits for them, and re-layouts  111 us (18%)
  matrix products  36.7 us (6%)
  starting transfers between devices  32.3 us (5%)
  blocking collectives  28.4 us (5%)
  other arithmetic  19.1 us (3%)
    all_to_all x1, waiting for transfers between devices, in_one_piece_2(): lax.all_to_all(both, axis, split_axis=split_dim, concat_axis=concat_dim,...  362 us
    all_to_all x1, blocking collectives, body(): lax.all_to_all(attended, 'head', split_axis=0, concat_axis=1, tiled=True)  28.4 us
    gather x4, local copies, waits for them, and re-layouts, attend(): got_keys[place_row]  19.9 us
    gather x4, local copies, waits for them, and re-layouts, attend(): got_values[place_row]  19.9 us
    sub x4, matrix products, attend(): weights = jnp.exp(scores - row_top)  18.9 us
    dot_general x4, matrix products, attend(): jnp.einsum('gmik,kgd->igmd', probability, value_block_rows, preferred_ele...  16.8 us
    all_to_all x1, starting transfers between devices, copy_for_each(): lax.all_to_all(jnp.broadcast_to(array[None], (count, *array.shape)), axis...  13.1 us
    reshape x1, local copies, waits for them, and re-layouts, body(): got_values.reshape(seq_count * CAP, BLOCK_ROWS, kv_heads_dev, HEAD_SIZE)  12.5 us
  transfers between devices with their start and end apart: 5, of which 3 were waited for; matrix products, arithmetic and copies ran while one was open for 9% of the time, Pallas kernels for 0%

commit v1 on v0

v1 whole, which is shorter than its diff:
```python
import functools
import math

import jax
import jax.numpy as jnp
from jax import lax
from jax.experimental import pallas as pl
from jax.experimental.pallas import tpu as pltpu
from jax.sharding import PartitionSpec as P

MESH = pl.DeviceIdType.MESH
ROWS = 128
D = 128
NX, NY, NZ = 4, 4, 8
GROUP = 8
SEL = 8
HELD = NZ * GROUP
GQ = 8
FAST = 22
SCALE2 = math.log2(math.e) / math.sqrt(D)


def kernel(U, place_ref, live_ref, list_ref, q_ref, k_ref, v_ref, out_ref,
           qbuf, kz, vz, ku, vu, pack, krl, vrl, cat, pbuf, obuf,
           ex_send, ex_recv, z_send, z_recv, b_send, b_recv, o_send, o_recv, loc):
    H = U // 2
    s = lax.axis_index("seq")
    x = lax.axis_index("head")
    c = s % 2
    y = (s // 2) % NY
    z = s // (2 * NY)
    a = x * (1 - c) + y * c
    b = y * (1 - c) + x * c
    g = a + 4 * c
    me = 2 * a + c

    def dev(xx, yy, zz, cc):
        return ((zz * NY + yy) * 2 + cc, xx)

    def dev_ab(aa, bb, zz, cc):
        return dev(aa * (1 - c) + bb * c, bb * (1 - c) + aa * c, zz, cc)

    def remote(src, dst, send, recv, target):
        return pltpu.make_async_remote_copy(src_ref=src, dst_ref=dst, send_sem=send, recv_sem=recv,
                                            device_id=target, device_id_type=MESH)

    barrier = pltpu.get_barrier_semaphore()

    def greet(target):
        pl.semaphore_signal(barrier, inc=1, device_id=target, device_id_type=MESH)

    greet(dev(x, y, z, 1 - c))
    for i in range(1, 4):
        for cc in range(2):
            greet(dev((x + i) % NX, y, z, cc))
            greet(dev(x, (y + i) % NY, z, cc))
    greet(dev(x, y, (z + 1) % NZ, c))
    greet(dev(x, y, (z + 7) % NZ, c))
    pl.semaphore_wait(barrier, 15)

    kinds = ((k_ref, kz, D), (v_ref, vz, D), (q_ref, qbuf, GQ * D))

    def piece(kind, t, i):
        src, dst, width = kinds[kind]
        other = (x + i) % NX if t == 0 else (y + i) % NY
        head = other + 4 * t
        slot = (2 * x + c) if t == 0 else (2 * y + c)
        at = slot if kind == 2 else z * GROUP + slot
        target = dev(other, y, z, 0) if t == 0 else dev(x, other, z, 1)
        src = src.at[:, pl.ds(pl.multiple_of(head * width, width), width)]
        return src, dst.at[at], kind, t * 4 + i, slot, target

    def send_piece(kind, t, i):
        src, dst, kind, n, slot, target = piece(kind, t, i)
        remote(src, dst, ex_send.at[kind, n], ex_recv.at[kind, slot], target).start()

    def each_piece(kind, go_remote, go_local):
        for i in (2, 1, 3):
            for t in range(2):
                go_remote(kind, t, i)
        for t in range(2):
            @pl.when(c == t)
            def _():
                go_local(kind, t)

            @pl.when(c != t)
            def _():
                go_remote(kind, t, 0)

    def local_piece(kind, t):
        src, dst, _, _, _, _ = piece(kind, t, 0)
        return pltpu.make_async_copy(src, dst, loc.at[kind])

    for kind in range(3):
        each_piece(kind, send_piece, lambda kind, t: local_piece(kind, t).start())

    def wait_exchange(kind):
        _, dst, _ = kinds[kind]

        def one(i, cc):
            aa = (a + i) % 4
            slot = 2 * aa + cc
            at = slot if kind == 2 else z * GROUP + slot
            remote(dst.at[at], dst.at[at], ex_send.at[kind, 0], ex_recv.at[kind, slot], dev_ab(aa, b, z, cc)).wait_recv()

        for i in range(1, 4):
            for cc in range(2):
                one(i, cc)
        one(0, 1 - c)
        for t in range(2):
            @pl.when(c == t)
            def _():
                local_piece(kind, t).wait()

    def z_copy(kind, way, step, receive):
        buf = (kz, vz)[kind]
        hop = step if receive else step - 1
        chunk = (z - hop + NZ) % NZ if way == 0 else (z + hop) % NZ
        first, count = (0, GROUP) if step < 4 else ((0, GROUP // 2) if way == 0 else (GROUP // 2, GROUP // 2))
        part = buf.at[pl.ds(chunk * GROUP + first, count)]
        target = dev(x, y, (z + 1) % NZ if way == 0 else (z + 7) % NZ, c)
        return remote(part, part, z_send.at[kind, way, step - 1], z_recv.at[kind, way, step - 1], target)

    def z_start(kind, step):
        for way in range(2):
            z_copy(kind, way, step, False).start()

    def z_wait(kind, step):
        for way in range(2):
            z_copy(kind, way, step, True).wait_recv()

    up = dev_ab(a, (b + 1) % 4, z, c)
    down = dev_ab(a, (b + 3) % 4, z, c)

    def b_copy(kind, n):
        have = (ku, vu)[kind]
        rel = (krl, vrl)[kind]
        src, dst, target = (
            (pack.at[pl.ds(0, U)], have.at[pl.ds(HELD, U)], up),
            (pack.at[pl.ds(2 * U, U)], have.at[pl.ds(HELD + 2 * U, U)], down),
            (pack.at[pl.ds(U, H)], rel.at[pl.ds(0, H)], up),
            (pack.at[pl.ds(U + H, H)], rel.at[pl.ds(H, H)], down),
            (rel.at[pl.ds(0, H)], have.at[pl.ds(HELD + U, H)], up),
            (rel.at[pl.ds(H, H)], have.at[pl.ds(HELD + U + H, H)], down),
        )[n]
        return remote(src, dst, b_send.at[kind, n], b_recv.at[kind, n], target)

    def b_begin(kind):
        held = (kz, vz)[kind]
        have = (ku, vu)[kind]
        keep = pltpu.make_async_copy(held, have.at[pl.ds(0, HELD)], loc.at[3 + kind])
        keep.start()

        def one(r, _):
            pack[r] = held[list_ref[r]]
            return 0

        lax.fori_loop(0, 3 * U, one, 0)
        for n in (2, 3, 0, 1):
            b_copy(kind, n).start()

    def b_relay(kind):
        for n in (2, 3):
            b_copy(kind, n).wait_recv()
            b_copy(kind, n + 2).start()

    def b_end(kind):
        for n in (0, 1, 4, 5):
            b_copy(kind, n).wait_recv()
        held = (kz, vz)[kind]
        have = (ku, vu)[kind]
        pltpu.make_async_copy(held, have.at[pl.ds(0, HELD)], loc.at[3 + kind]).wait()

    def b_sent(kind):
        for n in range(6):
            b_copy(kind, n).wait_send()

    row = lax.broadcasted_iota(jnp.int32, (2 * ROWS, ROWS), 0) % ROWS
    col = lax.broadcasted_iota(jnp.int32, (2 * ROWS, ROWS), 1)
    seen = col <= row

    def scores(m, _):
        for e in range(SEL):
            cat[e * ROWS : (e + 1) * ROWS, :] = ku[place_ref[m * SEL + e]]
        live = live_ref[m]
        bias = [jnp.where(e < live, 0.0, -jnp.inf).astype(jnp.float32) for e in range(SEL)]

        def heads(h, _):
            two = qbuf[m, :, pl.ds(pl.multiple_of(h * 2 * D, 2 * D), 2 * D)]
            two = jnp.concatenate([two[:, :D], two[:, D:]], axis=0)
            sc = lax.dot_general(two, cat[...], (((1,), (1,)), ((), ())), preferred_element_type=jnp.float32)
            parts = [jnp.where(seen, sc[:, :ROWS], -jnp.inf)]
            parts += [sc[:, e * ROWS : (e + 1) * ROWS] + bias[e] for e in range(1, SEL)]
            top = functools.reduce(jnp.maximum, parts)
            top = jnp.max(top, axis=1, keepdims=True)
            parts = [jnp.exp2((p - top) * SCALE2) for p in parts]
            total = jnp.sum(functools.reduce(jnp.add, parts), axis=1, keepdims=True)
            inv = 1.0 / total
            at = pl.ds(pl.multiple_of(h * 2 * ROWS, 2 * ROWS), 2 * ROWS)
            for e in range(SEL):
                pbuf[m, at, e * ROWS : (e + 1) * ROWS] = (parts[e] * inv).astype(jnp.bfloat16)
            return 0

        lax.fori_loop(0, GQ // 2, heads, 0)
        return 0

    def out_copy(t):
        i, cc = t // 2, t % 2
        aa = (a + i) % 4
        m = 2 * aa + cc
        src = obuf.at[m]
        dst = out_ref.at[:, pl.ds(pl.multiple_of(g * GQ * D, GQ * D), GQ * D)]
        return m, src, dst, remote(src, dst, o_send.at[t], o_recv.at[g], dev_ab(aa, b, z, cc))

    def attend(n, _):
        t = 7 - n
        m, src, dst, far = out_copy(t)
        for e in range(SEL):
            cat[e * ROWS : (e + 1) * ROWS, :] = vu[place_ref[m * SEL + e]]

        def heads(h, _):
            at = pl.ds(pl.multiple_of(h * 2 * ROWS, 2 * ROWS), 2 * ROWS)
            o = jnp.dot(pbuf[m, at, :], cat[...], preferred_element_type=jnp.float32).astype(jnp.bfloat16)
            first = pl.multiple_of(h * 2 * D, 2 * D)
            obuf[m, :, pl.ds(first, D)] = o[:ROWS]
            obuf[m, :, pl.ds(pl.multiple_of(first + D, D), D)] = o[ROWS:]
            return 0

        lax.fori_loop(0, GQ // 2, heads, 0)

        @pl.when(t == c)
        def _():
            pltpu.make_async_copy(src, dst, loc.at[5]).start()

        @pl.when(t != c)
        def _():
            far.start()

        return 0

    wait_exchange(0)
    z_start(0, 1)
    for step in range(1, 4):
        z_wait(0, step)
        z_start(0, step + 1)
    wait_exchange(1)
    z_wait(0, 4)
    z_start(1, 1)
    b_begin(0)
    b_relay(0)
    for step in range(1, 4):
        z_wait(1, step)
        z_start(1, step + 1)
    wait_exchange(2)
    b_end(0)
    b_sent(0)
    lax.fori_loop(0, 2, scores, 0)
    z_wait(1, 4)
    b_begin(1)
    lax.fori_loop(2, 4, scores, 0)
    b_relay(1)
    lax.fori_loop(4, 8, scores, 0)
    b_end(1)
    lax.fori_loop(0, 8, attend, 0)

    for kind in range(3):
        def sent(kind, t, i):
            src, dst, kind, n, slot, target = piece(kind, t, i)
            remote(src, dst, ex_send.at[kind, n], ex_recv.at[kind, slot], target).wait_send()

        each_piece(kind, sent, lambda kind, t: None)
    for kind in range(2):
        for step in range(1, 5):
            for way in range(2):
                z_copy(kind, way, step, False).wait_send()
    b_sent(1)
    for t in range(8):
        m, src, dst, far = out_copy(t)

        if t < 2:
            @pl.when(c != t)
            def _():
                far.wait_send()

            @pl.when(c == t)
            def _():
                pltpu.make_async_copy(src, dst, loc.at[5]).wait()
        else:
            far.wait_send()
    for h in range(8):
        dst = out_ref.at[:, pl.ds(h * GQ * D, GQ * D)]
        source = dev(h % 4, y, z, 0) if h < 4 else dev(x, h % 4, z, 1)

        @pl.when(g != h)
        def _():
            remote(dst, dst, o_send.at[0], o_recv.at[h], source).wait_recv()


def attention(U, ident, place, live, lists, queries, keys, values):
    any_space = pl.BlockSpec(memory_space=pl.ANY)
    smem = pl.BlockSpec(memory_space=pltpu.SMEM)
    block = (ROWS, D)
    bf16 = jnp.bfloat16
    dma = pltpu.SemaphoreType.DMA
    return pl.pallas_call(
        functools.partial(kernel, U),
        out_shape=jax.ShapeDtypeStruct(queries.shape, bf16),
        in_specs=[smem] * 3 + [any_space] * 3,
        out_specs=any_space,
        scratch_shapes=[
            pltpu.VMEM((GROUP, ROWS, GQ * D), bf16),
            pltpu.VMEM((HELD, *block), bf16),
            pltpu.VMEM((HELD, *block), bf16),
            pltpu.VMEM((HELD + 3 * U, *block), bf16),
            pltpu.VMEM((HELD + 3 * U, *block), bf16),
            pltpu.VMEM((3 * U, *block), bf16),
            pltpu.VMEM((U, *block), bf16),
            pltpu.VMEM((U, *block), bf16),
            pltpu.VMEM((SEL * ROWS, D), bf16),
            pltpu.VMEM((GROUP, GQ * ROWS, SEL * ROWS), bf16),
            pltpu.VMEM((GROUP, ROWS, GQ * D), bf16),
            dma((3, 8)), dma((3, 8)),
            dma((2, 2, 4)), dma((2, 2, 4)),
            dma((2, 6)), dma((2, 6)),
            dma((8,)), dma((8,)),
            dma((6,)),
        ],
        compiler_params=pltpu.CompilerParams(
            collective_id=ident, has_side_effects=True, vmem_limit_bytes=61 * 1024 * 1024),
    )(place, live, lists, queries, keys, values)


def body(queries, keys, values, selected, counts, block_slot):
    s = lax.axis_index("seq")
    x = lax.axis_index("head")
    c = s % 2
    y = (s // 2) % NY
    z = s // (2 * NY)
    b = jnp.where(c == 0, y, x)
    table = jnp.concatenate([selected, counts[:, None], block_slot[:, None]], axis=1)
    table = lax.all_gather(table, "seq", axis=0, tiled=True)
    sel, count, slots = table[:, :SEL], table[:, SEL], table[:, SEL + 1]
    nb = sel.shape[0]
    ids = jnp.arange(nb, dtype=jnp.int32)
    hit = (sel.reshape(-1)[:, None] == ids[None, :]).astype(jnp.bfloat16)
    slot = jnp.dot(hit, slots.astype(jnp.bfloat16)[:, None], preferred_element_type=jnp.float32)
    slot = slot.astype(jnp.int32).reshape(nb, SEL)
    slot = jnp.where(jnp.arange(SEL, dtype=jnp.int32)[None, :] < count[:, None], slot, -1)

    want = jnp.any(slot[:, :, None] == ids[None, None, :], axis=1)
    want = want.reshape(NZ, NY, 2, NX, nb)
    same_y = jnp.any(want, axis=(2, 3)).reshape(NZ * NY, NZ, NY, 2 * NX)
    same_x = jnp.any(want, axis=(1, 2)).reshape(NZ * NX, NZ * NY * 2, NX)
    n_y = jnp.sum(same_y.astype(jnp.int32), axis=(1, 3)).reshape(NZ, NY, NY)
    n_x = jnp.sum(same_x.astype(jnp.int32), axis=1).reshape(NZ, NX, NX)
    apart = jnp.arange(NY)[:, None] != jnp.arange(NY)[None, :]
    most = jnp.max(jnp.where(apart[None], jnp.maximum(n_y, n_x), 0))

    mine = lax.dynamic_slice_in_dim(slot.reshape(NZ, NY, 2, NX, SEL), z, 1, 0)[0]
    live = lax.dynamic_slice_in_dim(count.reshape(NZ, NY, 2, NX), z, 1, 0)[0]

    def arrange(t):
        rest = t.shape[3:]
        along_x = jnp.swapaxes(t, 1, 2).reshape(NY, GROUP, *rest)
        along_y = jnp.moveaxis(t, 2, 0).reshape(NX, GROUP, *rest)
        return jnp.where(c == 0, along_x, along_y)

    groups = arrange(mine).reshape(4, GROUP * SEL)
    sx, so = groups % NX, groups // NX
    sc, sy, sz = so % 2, (so // 2) % NY, so // (2 * NY)
    sa, sb = jnp.where(c == 0, sx, sy), jnp.where(c == 0, sy, sx)
    local = sz * GROUP + 2 * sa + sc
    sb = jnp.where(groups < 0, -1, sb)
    held = jnp.arange(HELD, dtype=jnp.int32)
    order = jnp.arange(4, dtype=jnp.int32)
    hits = (local[:, None, :, None] == held) & (sb[:, None, :, None] == order[None, :, None, None])
    wanted = jnp.any(hits, axis=2).astype(jnp.int32)
    earlier = (held[:, None] < held[None, :]).astype(jnp.int32)
    rank = jnp.sum(wanted[..., :, None] * earlier, axis=2)
    own = lax.dynamic_index_in_dim(rank, b, 0, False)
    out_rank = lax.dynamic_index_in_dim(rank, b, 1, False)
    out_want = lax.dynamic_index_in_dim(wanted, b, 1, False)
    entry_l = lax.dynamic_index_in_dim(local, b, 0, False)
    entry_b = lax.dynamic_index_in_dim(sb, b, 0, False)
    pick = ((entry_l[:, None] == held)[:, None, :] & (entry_b[:, None] == order)[:, :, None])
    entry_rank = jnp.sum(jnp.where(pick, own[None], 0), axis=(1, 2))
    gap = (b - entry_b + 4) % 4

    def place_of(U):
        far = HELD + (gap - 1) * U + entry_rank
        at = jnp.where(entry_b == b, entry_l, far)
        return jnp.where(entry_b < 0, 0, jnp.clip(at, 0, HELD + 3 * U - 1))

    live_mine = lax.dynamic_index_in_dim(arrange(live), b, 0, False)

    def list_of(U):
        r = jnp.arange(U, dtype=jnp.int32)
        chosen = (out_want[:, None, :] > 0) & (out_rank[:, None, :] == r[None, :, None])
        full = jnp.sum(jnp.where(chosen, held[None, None, :], 0), axis=2)
        turned = [lax.dynamic_index_in_dim(full, (b + j) % 4, 0, False) for j in (1, 2, 3)]
        return jnp.concatenate(turned)

    def run(U, ident):
        return lambda: attention(U, ident, place_of(U), live_mine, list_of(U), queries, keys, values)

    return lax.cond(most <= FAST, run(FAST, 0), run(HELD, 1))


def solution(mesh):
    return jax.shard_map(
        body,
        mesh=mesh,
        in_specs=(
            P(("seq", "head"), None),
            P(("seq", "head"), None),
            P(("seq", "head"), None),
            P("seq", None),
            P("seq"),
            P("seq"),
        ),
        out_specs=P(("seq", "head"), None),
        check_vma=False,
    )
```

time: 613 us -> 184 us (0.30)
  the two profiles are of different devices: /device:TPU:1 before, /device:TPU:10 now
where the time goes in v1:
time: 184 us
  Pallas kernels  114 us (62%)
  blocking collectives  52.6 us (29%)
  local copies, waits for them, and re-layouts  9.81 us (5%)
  other arithmetic  5.78 us (3%)
    pallas_call x1, Pallas kernels, attention(): pl.pallas_call(functools.partial(kernel, U), out_shape=jax.ShapeDtypeStru...  114 us
    all_gather x1, blocking collectives, body(): table = lax.all_gather(table, 'seq', axis=0, tiled=True)  52.6 us
    unnamed x9, local copies, waits for them, and re-layouts  4.63 us

profile of v1, /device:TPU:10, one launch (start us, length us, event | category | flops | bytes accessed | tf_op | source)
XLA Modules:
  0.0 184.0 jit_solution(11040596567651395327)
XLA Ops:
  0.0 0.7 copy.92
  0.8 0.7 copy.93
  1.5 0.8 add_bitcast_fusion
  2.3 52.6 %all-gather = s32[64,4,10]{2,1,0:T(4,128)S(1)} all-gather(s32[1,4,10]{2,1,0:T(4,128)S(1)} %add_bitcast_fusion), channel_id=1, replica_groups=mesh['seq'=64,'head'=4] {'seq'}, dimensions={0}, use_global_device_ids=true | all-gather | bytes 10400 | tf_op jit(solution)/shard_map/all_gather | solution.py:341
  54.9 0.1 eq.162
  55.0 0.5 broadcast.420
  55.5 0.8 fusion.30
  56.6 0.5 fusion.12
  57.1 0.1 lt.148
  57.3 0.2 reshape.277
  57.8 0.1 iota_compare_fusion.5
  57.9 0.2 and_reduce_fusion
  58.2 0.2 multiply_reduce_fusion
  58.5 0.1 fusion.14
  58.6 0.7 fusion.11
  59.4 0.1 fusion.28
  59.6 0.7 reshape.282
  60.3 0.6 reduce_sum.54
  60.9 1.1 reshape.283
  62.0 0.1 reduce_sum.55
  62.1 0.1 copy.109
  62.3 0.6 select_reduce_fusion.4
  63.6 117.3 %conditional.1 = (bf16[128,8192]{1,0:T(8,128)(2,1)}) conditional(s32[]{:T(128)} %convert_element_type.41, (s32[64]{0:T(128)S(1)}, s32[]{:T(128)}, s32[64]{0:T(128)S(1)}, s32[64]{0:T(128)S(1)}, s32[64]{0:T(128)S(1)}, /*index=5*/s32[4,4,64]{2,1,0:T(4,128)S(1)}, s32[4,4,64]{2,1,0:T(4,128)S(1)}, s32[64]{0:T(128)S(1)}, pred[]{:T(512)}, ...), branch_computations={%region_9.11_spmd.clone, %region_11.13_spmd.clone} | conditional | flops 120333 | bytes 59074 | solution.py:406
  63.7 0.1 copy.108
  63.8 0.8 dynamic-slice_reduce_fusion.4.live_ref
  64.6 0.2 select_reduce_fusion.2
  64.8 0.5 compare_select_fusion.3.place_ref
  65.4 0.4 select_reduce_fusion.3
  65.8 0.2 dynamic-slice_reduce_fusion.3
  66.1 0.6 pad_add_fusion.1.list_ref
  66.7 114.0 %branch_1_fun.1 = bf16[128,8192]{1,0:T(8,128)(2,1)} custom-call(s32[64]{0:T(128)} %compare_select_fusion.3.place_ref, s32[8]{0:T(128)} %dynamic-slice_reduce_fusion.4.live_ref, s32[66]{0:T(128)} %pad_add_fusion.1.list_ref, bf16[128,8192]{1,0:T(8,128)(2,1)S(1)} %get-tuple-element.267.q_ref, bf16[128,1024]{1,0:T(8,128)(2,1)S(1)} %get-tuple-element.268.k_ref, ...), custom_call_target="tpu_custom_call" | custom-call | tf_op jit(solution)/shard_map/cond/branch_1_fun/pallas_call | solution.py:305
  180.9 3.1 %copy.121 = bf16[128,8192]{1,0:T(8,128)(2,1)} copy(bf16[128,8192]{1,0:T(8,128)(2,1)} %get-tuple-element.80) | data formatting | bytes 4194304
  (41 shorter events, 0.9 us)
Async XLA Ops:
  58.5 5.0 %copy-start = (bf16[128,8192]{1,0:T(8,128)(2,1)S(1)}, bf16[128,8192]{1,0:T(8,128)(2,1)}, u32[]{:S(2)}) copy-start(bf16[128,8192]{1,0:T(8,128)(2,1)} %param.8) | copy-start | bytes 6291460
  58.5 5.0 %copy-start.1 = (bf16[128,1024]{1,0:T(8,128)(2,1)S(1)}, bf16[128,1024]{1,0:T(8,128)(2,1)}, u32[]{:S(2)}) copy-start(bf16[128,1024]{1,0:T(8,128)(2,1)} %param.9) | copy-start | bytes 786436

commit v2 on v1

v2 whole, which is shorter than its diff:
```python
import functools
import math

import jax
import jax.numpy as jnp
from jax import lax
from jax.experimental import pallas as pl
from jax.experimental.pallas import tpu as pltpu
from jax.sharding import PartitionSpec as P

MESH = pl.DeviceIdType.MESH
ROWS = 128
D = 128
NX, NY, NZ = 4, 4, 8
GROUP = 8
SEL = 8
HELD = NZ * GROUP
GQ = 8
FAST = (16, 12)
NEAR, AFAR = 5 * GROUP, 3 * GROUP
FULL = (NEAR, AFAR)
TW = 64
SCALE2 = math.log2(math.e) / math.sqrt(D)


def kernel(U, key_ref, slot_ref, q_ref, k_ref, v_ref, out_ref, flag_ref,
           qbuf, kn, kf, vn, vf, ku, vu, pack, krl, vrl, cat, pbuf, obuf, orl, keyt, slott, wants, index, smem, flags,
           ex_send, ex_recv, z_send, z_recv, b_send, b_recv, o_send, o_recv, r_recv, t_send, t_recv, loc):
    s = lax.axis_index("seq")
    x = lax.axis_index("head")
    c = s % 2
    y = (s // 2) % NY
    z = s // (2 * NY)
    a = x * (1 - c) + y * c
    b = y * (1 - c) + x * c
    g = a + 4 * c
    r0 = y * 2 + c

    def dev(xx, yy, zz, cc):
        return ((zz * NY + yy) * 2 + cc, xx)

    def dev_ab(aa, bb, zz, cc):
        return dev(aa * (1 - c) + bb * c, bb * (1 - c) + aa * c, zz, cc)

    def remote(src, dst, send, recv, target):
        return pltpu.make_async_remote_copy(src_ref=src, dst_ref=dst, send_sem=send, recv_sem=recv,
                                            device_id=target, device_id_type=MESH)

    barrier = pltpu.get_barrier_semaphore()

    def greet(target):
        pl.semaphore_signal(barrier, inc=1, device_id=target, device_id_type=MESH)

    greet(dev(x, y, z, 1 - c))
    for i in range(1, 4):
        for cc in range(2):
            greet(dev((x + i) % NX, y, z, cc))
            greet(dev(x, (y + i) % NY, z, cc))
    for i in range(1, NZ):
        greet(dev(x, y, (z + i) % NZ, c))
    pl.semaphore_wait(barrier, 20)

    def t_copy(n, receive):
        other = (r0 + n) % 8
        row = other if receive else r0
        target = dev(x, other // 2, z, other % 2)
        sem = (8 - n) % 8 if receive else n
        return (
            remote(key_ref, keyt.at[row], t_send.at[0, n], t_recv.at[0, sem], target),
            remote(slot_ref, slott.at[z, pl.ds(row, 1)], t_send.at[1, n], t_recv.at[1, sem], target),
        )

    def tz_copy(kind, n, receive):
        other = (z + n) % NZ
        row = other if receive else z
        sem = (8 - n) % 8 if receive else n
        buf = (slott, flags)[kind]
        return remote(buf.at[row], buf.at[row], t_send.at[2 + kind, n], t_recv.at[2 + kind, sem], dev(x, y, other, c))

    def t_local():
        return (pltpu.make_async_copy(key_ref, keyt.at[r0], loc.at[6]),
                pltpu.make_async_copy(slot_ref, slott.at[z, pl.ds(r0, 1)], loc.at[7]))

    kinds = ((k_ref, kn, D), (v_ref, vn, D), (q_ref, qbuf, GQ * D))

    def piece(kind, t, i):
        src, dst, width = kinds[kind]
        other = (x + i) % NX if t == 0 else (y + i) % NY
        head = other + 4 * t
        slot = (2 * x + c) if t == 0 else (2 * y + c)
        target = dev(other, y, z, 0) if t == 0 else dev(x, other, z, 1)
        src = src.at[:, pl.ds(pl.multiple_of(head * width, width), width)]
        return src, dst.at[slot], kind, t * 4 + i, slot, target

    def send_piece(kind, t, i):
        src, dst, kind, n, slot, target = piece(kind, t, i)
        remote(src, dst, ex_send.at[kind, n], ex_recv.at[kind, slot], target).start()

    def each_piece(kind, go_remote, go_local):
        for i in (2, 1, 3):
            for t in range(2):
                go_remote(kind, t, i)
        for t in range(2):
            @pl.when(c == t)
            def _():
                go_local(kind, t)

            @pl.when(c != t)
            def _():
                go_remote(kind, t, 0)

    def local_piece(kind, t):
        src, dst, _, _, _, _ = piece(kind, t, 0)
        return pltpu.make_async_copy(src, dst, loc.at[kind])

    def exchange(kind):
        each_piece(kind, send_piece, lambda kind, t: local_piece(kind, t).start())

    def wait_exchange(kind):
        _, dst, _ = kinds[kind]

        def one(i, cc):
            aa = (a + i) % 4
            slot = 2 * aa + cc
            remote(dst.at[slot], dst.at[slot], ex_send.at[kind, 0], ex_recv.at[kind, slot], dev_ab(aa, b, z, cc)).wait_recv()

        for i in range(1, 4):
            for cc in range(2):
                one(i, cc)
        one(0, 1 - c)
        for t in range(2):
            @pl.when(c == t)
            def _():
                local_piece(kind, t).wait()

    HALF = GROUP // 2

    def z_part(kind, way, hop, sub):
        near, far = ((kn, kf), (vn, vf))[kind]
        at = ((0, 4, 3, 2, 1), (0, 1, 2, 0, 1))[way][hop] * GROUP + sub * HALF
        return (near if hop <= 2 else far).at[pl.ds(at, HALF)]

    def z_copy(kind, way, step, sub):
        target = dev(x, y, (z + 1) % NZ if way == 0 else (z + 7) % NZ, c)
        return remote(z_part(kind, way, step - 1, sub), z_part(kind, way, step, sub),
                      z_send.at[kind, way, step - 1, sub], z_recv.at[kind, way, step - 1, sub], target)

    def z_parts(step):
        return [(way, sub) for sub in range(2) for way in range(2) if step < 4 or way == sub]

    def z_first(kind):
        for way, sub in z_parts(1):
            z_copy(kind, way, 1, sub).start()

    def z_hop(kind, step):
        for way, sub in z_parts(step):
            z_copy(kind, way, step, sub).wait_recv()
            if (way, sub) in z_parts(step + 1) and step < 4:
                z_copy(kind, way, step + 1, sub).start()

    up = dev_ab(a, (b + 1) % 4, z, c)
    down = dev_ab(a, (b + 3) % 4, z, c)
    total_u = U[0] + U[1]

    def b_copy(kind, part, n):
        have = (ku, vu)[kind]
        rel = (krl, vrl)[kind]
        u = U[part]
        h = u // 2
        p = 3 * U[0] * part
        f = HELD + p
        l = U[0] * part
        src, dst, target = (
            (pack.at[pl.ds(p, u)], have.at[pl.ds(f, u)], up),
            (pack.at[pl.ds(p + 2 * u, u)], have.at[pl.ds(f + 2 * u, u)], down),
            (pack.at[pl.ds(p + u, h)], rel.at[pl.ds(l, h)], up),
            (pack.at[pl.ds(p + u + h, h)], rel.at[pl.ds(l + h, h)], down),
            (rel.at[pl.ds(l, h)], have.at[pl.ds(f + u, h)], up),
            (rel.at[pl.ds(l + h, h)], have.at[pl.ds(f + u + h, h)], down),
        )[n]
        return remote(src, dst, b_send.at[kind, part, n], b_recv.at[kind, part, n], target)

    def b_begin(kind, part):
        held = ((kn, kf), (vn, vf))[kind][part]
        u = U[part]
        p = 3 * U[0] * part
        base, size = (0, NEAR) if part == 0 else (NEAR, AFAR)

        def one(r, _):
            for j in range(3):
                pack[p + j * u + r] = held[jnp.clip(smem[2, (j + 1) * TW + U[0] * part + r] - base, 0, size - 1)]
            return 0

        lax.fori_loop(0, u, one, 0)
        for n in (2, 3, 0, 1):
            b_copy(kind, part, n).start()

    def b_relay(kind, part):
        for n in (2, 3):
            b_copy(kind, part, n).wait_recv()
            b_copy(kind, part, n + 2).start()

    def b_end(kind, part):
        for n in (0, 1, 4, 5):
            b_copy(kind, part, n).wait_recv()

    def keep(kind, part):
        held = ((kn, kf), (vn, vf))[kind][part]
        at = pl.ds(0, NEAR) if part == 0 else pl.ds(NEAR, AFAR)
        return pltpu.make_async_copy(held, (ku, vu)[kind].at[at], loc.at[9 + 2 * kind + part])

    def b_sent(kind):
        for part in range(2):
            for n in range(6):
                b_copy(kind, part, n).wait_send()

    def near_far(t):
        far = (t // 32 - z + NZ) % NZ
        return (far >= 3) & (far <= 5)

    def lists():
        f32, bf16, i32 = jnp.float32, jnp.bfloat16, jnp.int32
        n = NZ * NY * 2 * NX

        def one(hit):
            return jnp.where(hit, 1.0, 0.0).astype(f32)

        t_lane = lax.broadcasted_iota(i32, (NZ * NY * 2, n), 1)
        slots = slott[...].reshape(NZ * NY * 2, D)
        perm = jnp.concatenate([one(slots[:, h : h + 1] == t_lane) for h in range(NX)], axis=0).astype(bf16)
        keys = keyt[...].reshape(n, D)
        lane = lax.broadcasted_iota(i32, (n, D), 1)
        named = jnp.concatenate([one(keys == lane), one(keys == lane + D)], axis=1).astype(bf16)
        entry = jnp.dot(named, perm, preferred_element_type=f32)
        block = jnp.max(entry.reshape(4 * GROUP, SEL, n), axis=1)
        by_y = jnp.max(block.reshape(NY, GROUP, n), axis=1)
        by_x = functools.reduce(jnp.maximum, [block[i * NX : (i + 1) * NX] for i in range(2 * NY)])
        want = jnp.concatenate([by_y, by_x], axis=0)
        t0 = lax.broadcasted_iota(i32, (n, n), 0)
        t1 = lax.broadcasted_iota(i32, (n, n), 1)
        before = (t0 < t1) & (near_far(t0) == near_far(t1))
        same_y = (t0 // 8) % NY == (t1 // 8) % NY
        same_x = t0 % NX == t1 % NX
        rank_y = jnp.dot(want.astype(bf16), one(before & same_y).astype(bf16), preferred_element_type=f32)
        rank_x = jnp.dot(want.astype(bf16), one(before & same_x).astype(bf16), preferred_element_type=f32)
        group = lax.broadcasted_iota(i32, (8, n), 0)
        t8 = lax.broadcasted_iota(i32, (8, n), 1)
        first = group < 4
        rank = jnp.where(first, rank_y, rank_x)
        away = jnp.where(first, (t8 // 8) % NY, t8 % NX) != group % 4
        room = jnp.where(near_far(t8), U[1], U[0]).astype(f32)
        over = one((want > 0.5) & away & (rank > room - 0.5))
        flags[z] = jnp.broadcast_to(jnp.max(over), (8, D)).astype(i32)
        wants[0] = want
        wants[1] = rank
        t = lax.broadcasted_iota(i32, (1, n), 1)
        tx, ty, tc, tz = t % NX, (t // 8) % NY, (t // 4) % 2, t // 32
        ta = tx * (1 - c) + ty * c
        tb = ty * (1 - c) + tx * c
        off = (tz - z + NZ) % NZ
        local = jnp.where(off <= 2, off, jnp.where(off >= 6, off - 3, off + 2)) * GROUP + 2 * ta + tc
        late = near_far(t)

        def row(d):
            at = pl.ds(4 * c + d, 1)
            return wants[0, at, :], wants[1, at, :].astype(i32)

        _, rk = row(b)
        gap = (b - tb + 4) % 4 - 1
        there = HELD + jnp.where(late, 3 * U[0] + gap * U[1], gap * U[0]) + rk
        at = jnp.clip(jnp.where(tb == b, local, there), 0, HELD + 3 * total_u - 1)
        r8 = lax.broadcasted_iota(i32, (8, n), 0)
        at8 = jnp.broadcast_to(at, (8, n))
        lhs = jnp.where(r8 == 0, at8 // 16, jnp.where(r8 == 1, at8 % 16, 1)).astype(f32).astype(bf16)
        got = lax.dot_general(lhs, entry.astype(bf16), (((1,), (1,)), ((), ())), preferred_element_type=f32)
        picks = []
        k = lax.broadcasted_iota(i32, (TW, n), 0)
        for j in range(4):
            wj, rj = row((b + j) % 4)
            kk = jnp.where((wj > 0.5) & (tb == b), rj + jnp.where(late, U[0], 0), -1)
            picks.append(one(kk == k))
        picks = jnp.concatenate(picks, axis=0).astype(bf16)
        names = jnp.broadcast_to(local, (8, n)).astype(f32).astype(bf16)
        chosen = lax.dot_general(names, picks, (((1,), (1,)), ((), ())), preferred_element_type=f32)
        place = got[0:1] * 16.0 + got[1:2]
        index[0:1, :] = place.astype(i32)
        index[1:2, :] = got[2:3].astype(i32)
        index[2:3, :] = chosen[0:1].astype(i32)

    def to_scalars():
        return pltpu.make_async_copy(index, smem, loc.at[8])

    def entry_at(m):
        aa, cc = m // 2, m % 2
        yy = y * (1 - c) + aa * c
        xx = aa * (1 - c) + x * c
        return ((yy * 2 + cc) * NX + xx) * SEL

    def gather_entries(src, m):
        first = entry_at(m)
        for e in range(SEL):
            cat[e * ROWS : (e + 1) * ROWS, :] = src[jnp.clip(smem[0, first + e], 0, HELD + 3 * total_u - 1)]
        return first

    row = lax.broadcasted_iota(jnp.int32, (2 * ROWS, ROWS), 0) % ROWS
    col = lax.broadcasted_iota(jnp.int32, (2 * ROWS, ROWS), 1)
    seen = col <= row

    def scores(m, _):
        first = gather_entries(ku, m)
        bias = [jnp.where(smem[1, first + e] > 0, 0.0, -jnp.inf).astype(jnp.float32) for e in range(SEL)]

        def heads(h, _):
            two = qbuf[m, :, pl.ds(pl.multiple_of(h * 2 * D, 2 * D), 2 * D)]
            two = jnp.concatenate([two[:, :D], two[:, D:]], axis=0)
            sc = lax.dot_general(two, cat[...], (((1,), (1,)), ((), ())), preferred_element_type=jnp.float32)
            parts = [jnp.where(seen, sc[:, :ROWS], -jnp.inf)]
            parts += [sc[:, e * ROWS : (e + 1) * ROWS] + bias[e] for e in range(1, SEL)]
            top = functools.reduce(jnp.maximum, parts)
            top = jnp.max(top, axis=1, keepdims=True)
            parts = [jnp.exp2((p - top) * SCALE2) for p in parts]
            total = jnp.sum(functools.reduce(jnp.add, parts), axis=1, keepdims=True)
            inv = 1.0 / total
            at = pl.ds(pl.multiple_of(h * 2 * ROWS, 2 * ROWS), 2 * ROWS)
            for e in range(SEL):
                pbuf[m, at, e * ROWS : (e + 1) * ROWS] = (parts[e] * inv).astype(jnp.bfloat16)
            return 0

        lax.fori_loop(0, GQ // 2, heads, 0)
        return 0

    def columns(head):
        return out_ref.at[:, pl.ds(pl.multiple_of(head * GQ * D, GQ * D), GQ * D)]

    def out_copy(i, cc):
        m = 2 * ((a + i) % 4) + cc
        return remote(obuf.at[m], columns(g), o_send.at[2 * i + cc], o_recv.at[g], dev_ab((a + i) % 4, b, z, cc))

    def out_via(cc):
        m = 2 * ((a + 2) % 4) + cc
        step = 1 if cc == 0 else 3
        return remote(obuf.at[m], orl.at[cc], o_send.at[4 + cc], r_recv.at[cc], dev_ab((a + step) % 4, b, z, c))

    def out_relay(cc):
        step = 1 if cc == 0 else 3
        source = (a + 4 - step) % 4 + 4 * c
        return remote(orl.at[cc], columns(source), o_send.at[8 + cc], o_recv.at[source], dev_ab((a + step) % 4, b, z, cc))

    def out_local():
        return pltpu.make_async_copy(obuf.at[2 * a + c], columns(g), loc.at[5])

    def attend(n, _):
        q = n // 2
        i = jnp.where(q < 2, 2 + q, 3 - q)
        cc = n % 2
        m = 2 * ((a + i) % 4) + cc
        gather_entries(vu, m)

        def heads(h, _):
            at = pl.ds(pl.multiple_of(h * 2 * ROWS, 2 * ROWS), 2 * ROWS)
            o = jnp.dot(pbuf[m, at, :], cat[...], preferred_element_type=jnp.float32).astype(jnp.bfloat16)
            first = pl.multiple_of(h * 2 * D, 2 * D)
            obuf[m, :, pl.ds(first, D)] = o[:ROWS]
            obuf[m, :, pl.ds(pl.multiple_of(first + D, D), D)] = o[ROWS:]
            return 0

        lax.fori_loop(0, GQ // 2, heads, 0)
        for k in range(2):
            @pl.when(n == k)
            def _():
                out_via(k).start()
        for q0, i0 in ((1, 3), (2, 1), (3, 0)):
            for k in range(2):
                @pl.when((n == 2 * q0 + k) & ((i0 > 0) | (c != k)))
                def _():
                    out_copy(i0, k).start()

        @pl.when(n == 6 + c)
        def _():
            out_local().start()

        @pl.when(n == 4)
        def _():
            for k in range(2):
                remote(orl.at[k], orl.at[k], o_send.at[4 + k], r_recv.at[k],
                       dev_ab((a + (3 if k == 0 else 1)) % 4, b, z, c)).wait_recv()
                out_relay(k).start()

        return 0

    exchange(0)
    for n in range(1, 8):
        for copy in t_copy(n, False):
            copy.start()
    for copy in t_local():
        copy.start()
    exchange(1)
    exchange(2)
    wait_exchange(0)
    z_first(0)
    for n in range(1, 8):
        for copy in t_copy(n, True):
            copy.wait_recv()
    for copy in t_local():
        copy.wait()
    for n in range(1, 8):
        tz_copy(0, n, False).start()
    z_hop(0, 1)
    for n in range(1, 8):
        tz_copy(0, n, True).wait_recv()
    lists()
    z_hop(0, 2)
    to_scalars().start()
    for n in range(1, 8):
        tz_copy(1, n, False).start()
    to_scalars().wait()
    b_begin(0, 0)
    z_hop(0, 3)
    wait_exchange(1)
    z_first(1)
    b_relay(0, 0)
    z_hop(0, 4)
    keep(0, 0).start()
    keep(0, 1).start()
    b_begin(0, 1)
    z_hop(1, 1)
    b_relay(0, 1)
    z_hop(1, 2)
    b_end(0, 0)
    wait_exchange(2)
    keep(0, 0).wait()
    keep(0, 1).wait()
    b_end(0, 1)
    b_sent(0)
    b_begin(1, 0)
    lax.fori_loop(0, 1, scores, 0)
    z_hop(1, 3)
    b_relay(1, 0)
    lax.fori_loop(1, 3, scores, 0)
    z_hop(1, 4)
    keep(1, 0).start()
    keep(1, 1).start()
    b_begin(1, 1)
    lax.fori_loop(3, 5, scores, 0)
    b_relay(1, 1)
    lax.fori_loop(5, 8, scores, 0)
    b_end(1, 0)
    keep(1, 0).wait()
    keep(1, 1).wait()
    b_end(1, 1)
    lax.fori_loop(0, 8, attend, 0)

    for n in range(1, 8):
        tz_copy(1, n, True).wait_recv()
    flag_ref[...] = functools.reduce(jnp.maximum, [flags[i] for i in range(NZ)])
    for n in range(1, 8):
        for copy in t_copy(n, False):
            copy.wait_send()
        for kind in range(2):
            tz_copy(kind, n, False).wait_send()
    for kind in range(3):
        def sent(kind, t, i):
            src, dst, kind, n, slot, target = piece(kind, t, i)
            remote(src, dst, ex_send.at[kind, n], ex_recv.at[kind, slot], target).wait_send()

        each_piece(kind, sent, lambda kind, t: None)
    for kind in range(2):
        for step in range(1, 5):
            for way, sub in z_parts(step):
                z_copy(kind, way, step, sub).wait_send()
    b_sent(1)
    for k in range(2):
        out_via(k).wait_send()
        out_relay(k).wait_send()
        for i in (1, 3):
            out_copy(i, k).wait_send()

        @pl.when(c != k)
        def _():
            out_copy(0, k).wait_send()
    out_local().wait()
    for h in range(8):
        dst = out_ref.at[:, pl.ds(h * GQ * D, GQ * D)]
        source = dev(h % 4, y, z, 0) if h < 4 else dev(x, h % 4, z, 1)

        @pl.when(g != h)
        def _():
            remote(dst, dst, o_send.at[0], o_recv.at[h], source).wait_recv()


def attention(U, ident, named, slots, queries, keys, values):
    any_space = pl.BlockSpec(memory_space=pl.ANY)
    vmem = pl.BlockSpec(memory_space=pltpu.VMEM)
    block = (ROWS, D)
    bf16 = jnp.bfloat16
    dma = pltpu.SemaphoreType.DMA
    near, far = U
    return pl.pallas_call(
        functools.partial(kernel, U),
        out_shape=(jax.ShapeDtypeStruct(queries.shape, bf16), jax.ShapeDtypeStruct((8, D), jnp.int32)),
        in_specs=[vmem] * 2 + [any_space] * 3,
        out_specs=(any_space, vmem),
        scratch_shapes=[
            pltpu.VMEM((GROUP, ROWS, GQ * D), bf16),
            pltpu.VMEM((NEAR, *block), bf16),
            pltpu.VMEM((AFAR, *block), bf16),
            pltpu.VMEM((NEAR, *block), bf16),
            pltpu.VMEM((AFAR, *block), bf16),
            pltpu.VMEM((HELD + 3 * (near + far), *block), bf16),
            pltpu.VMEM((HELD + 3 * (near + far), *block), bf16),
            pltpu.VMEM((3 * (near + far), *block), bf16),
            pltpu.VMEM((near + far, *block), bf16),
            pltpu.VMEM((near + far, *block), bf16),
            pltpu.VMEM((SEL * ROWS, D), bf16),
            pltpu.VMEM((GROUP, GQ * ROWS, SEL * ROWS), bf16),
            pltpu.VMEM((GROUP, ROWS, GQ * D), bf16),
            pltpu.VMEM((2, ROWS, GQ * D), bf16),
            pltpu.VMEM((8, 4 * SEL, D), jnp.int32),
            pltpu.VMEM((NZ, 8, D), jnp.int32),
            pltpu.VMEM((2, 8, 256), jnp.float32),
            pltpu.VMEM((8, 256), jnp.int32),
            pltpu.SMEM((8, 256), jnp.int32),
            pltpu.VMEM((NZ, 8, D), jnp.int32),
            dma((3, 8)), dma((3, 8)),
            dma((2, 2, 4, 2)), dma((2, 2, 4, 2)),
            dma((2, 2, 6)), dma((2, 2, 6)),
            dma((10,)), dma((8,)), dma((2,)),
            dma((4, 8)), dma((4, 8)),
            dma((13,)),
        ],
        compiler_params=pltpu.CompilerParams(
            collective_id=ident, has_side_effects=True, vmem_limit_bytes=61 * 1024 * 1024),
    )(named, slots, queries, keys, values)


def body(queries, keys, values, selected, counts, block_slot):
    live = jnp.arange(SEL, dtype=jnp.int32)[None, :] < counts[:, None]
    named = jnp.where(live, (selected % NX) * (NZ * NY * 2) + selected // NX, -1)
    named = jnp.broadcast_to(named.reshape(-1, 1), (4 * SEL, D))
    slots = jnp.pad(block_slot, (0, D - 4))[None, :]
    out, flag = attention(FAST, 0, named, slots, queries, keys, values)
    again = lambda: attention(FULL, 1, named, slots, queries, keys, values)[0]
    return lax.cond(flag[0, 0] > 0, again, lambda: out)


def solution(mesh):
    return jax.shard_map(
        body,
        mesh=mesh,
        in_specs=(
            P(("seq", "head"), None),
            P(("seq", "head"), None),
            P(("seq", "head"), None),
            P("seq", None),
            P("seq"),
            P("seq"),
        ),
        out_specs=P(("seq", "head"), None),
        check_vma=False,
    )
```

time: 184 us -> 104 us (0.57)
  the two profiles are of different devices: /device:TPU:10 before, /device:TPU:1 now
where the time goes in v2:
time: 104 us
  Pallas kernels  97.6 us (94%)
  local copies, waits for them, and re-layouts  5.25 us (5%)
    pallas_call x1, Pallas kernels, attention(): pl.pallas_call(functools.partial(kernel, U), out_shape=(jax.ShapeDtypeStr...  97.6 us
    unnamed x7, local copies, waits for them, and re-layouts  3.11 us

profile of v2, /device:TPU:1, one launch (start us, length us, event | category | flops | bytes accessed | tf_op | source)
XLA Modules:
  0.0 104.3 jit_solution(14745790692266389227)
XLA Ops:
  0.0 0.0 copy-start.2
  0.0 0.0 copy-start.1
  0.0 0.0 copy-start
  0.0 0.8 pad_bitcast_fusion.slot_ref
  0.8 0.8 fusion.2
  1.6 0.1 broadcast_in_dim.14
  1.7 0.1 broadcast_in_dim.15.key_ref
  1.7 97.6 %shard_map.66 = (bf16[128,8192]{1,0:T(8,128)(2,1)}, s32[8,128]{1,0:T(8,128)}) custom-call(s32[32,128]{1,0:T(8,128)S(1)} %broadcast_in_dim.15.key_ref, s32[1,128]{1,0:T(1,128)S(1)} %pad_bitcast_fusion.slot_ref, bf16[128,8192]{1,0:T(8,128)(2,1)} %q_ref.1, bf16[128,1024]{1,0:T(8,128)(2,1)} %k_ref.1, bf16[128,1024]{1,0:T(8,128)(2,1)} %v_ref.1), custom_call_target="tpu_custom_call" | custom-call | tf_op jit(solution)/shard_map/pallas_call | solution.py:498
  99.3 1.2 %slice.3 = s32[1,1]{1,0:T(1,128)} slice(s32[8,128]{1,0:T(8,128)} %get-tuple-element.27), slice={[0:1], [0:1]} | slice | bytes 8 | tf_op jit(solution)/shard_map/slice | solution.py:543
  101.1 0.0 copy-done.2
  101.1 0.0 copy-done.1
  101.2 0.0 copy-done
  101.2 3.1 %copy.12 = bf16[128,8192]{1,0:T(8,128)(2,1)} copy(bf16[128,8192]{1,0:T(8,128)(2,1)} %get-tuple-element.29) | data formatting | bytes 4194304
  (1 shorter events, 0.0 us)
Async XLA Ops:
  0.0 101.1 %copy-start.2 = (bf16[128,1024]{1,0:T(8,128)(2,1)S(1)}, bf16[128,1024]{1,0:T(8,128)(2,1)}, u32[]{:S(2)}) copy-start(bf16[128,1024]{1,0:T(8,128)(2,1)} %v_ref.1) | copy-start | bytes 786436
  0.0 101.1 %copy-start.1 = (bf16[128,1024]{1,0:T(8,128)(2,1)S(1)}, bf16[128,1024]{1,0:T(8,128)(2,1)}, u32[]{:S(2)}) copy-start(bf16[128,1024]{1,0:T(8,128)(2,1)} %k_ref.1) | copy-start | bytes 786436
  0.0 101.2 %copy-start = (bf16[128,8192]{1,0:T(8,128)(2,1)S(1)}, bf16[128,8192]{1,0:T(8,128)(2,1)}, u32[]{:S(2)}) copy-start(bf16[128,8192]{1,0:T(8,128)(2,1)} %q_ref.1) | copy-start | bytes 6291460

commit v3 on v2

--- a/solution.py
+++ b/solution.py
@@ -16,15 +16,15 @@
 SEL = 8
 HELD = NZ * GROUP
 GQ = 8
-FAST = (16, 12)
-NEAR, AFAR = 5 * GROUP, 3 * GROUP
-FULL = (NEAR, AFAR)
+FAST = (10, 6, 8)
+CLASSES = FULL = (5 * GROUP, 2 * GROUP, GROUP)
+STARTS = (0, CLASSES[0], CLASSES[0] + CLASSES[1])
 TW = 64
 SCALE2 = math.log2(math.e) / math.sqrt(D)
 
 
-def kernel(U, key_ref, slot_ref, q_ref, k_ref, v_ref, out_ref, flag_ref,
-           qbuf, kn, kf, vn, vf, ku, vu, pack, krl, vrl, cat, pbuf, obuf, orl, keyt, slott, wants, index, smem, flags,
+def kernel(U, sel_ref, count_ref, own_ref, q_ref, k_ref, v_ref, out_ref, flag_ref,
+           key_ref, slot_ref, qbuf, kn, km, kf, vn, vm, vf, ku, vu, kpack, vpack, krl, vrl, cat, pbuf, obuf, orl, keyt, slott, wants, index, smem, flags,
            ex_send, ex_recv, z_send, z_recv, b_send, b_recv, o_send, o_recv, r_recv, t_send, t_recv, loc):
     s = lax.axis_index("seq")
     x = lax.axis_index("head")
@@ -46,6 +46,22 @@
         return pltpu.make_async_remote_copy(src_ref=src, dst_ref=dst, send_sem=send, recv_sem=recv,
                                             device_id=target, device_id_type=MESH)
 
+    OFF = (0, U[0], U[0] + U[1])
+    total_u = sum(U)
+
+    row = lax.broadcasted_iota(jnp.int32, (4 * SEL, D), 0)
+    lane = lax.broadcasted_iota(jnp.int32, (1, D), 1)
+    names = jnp.full((4 * SEL, D), -1, jnp.int32)
+    spots = jnp.zeros((1, D), jnp.int32)
+    for h in range(NX):
+        for e in range(SEL):
+            block = sel_ref[h, e]
+            name = jnp.where(e < count_ref[h], (block % NX) * (NZ * NY * 2) + block // NX, -1)
+            names = jnp.where(row == h * SEL + e, name, names)
+        spots = jnp.where(lane == h, own_ref[h], spots)
+    key_ref[...] = names
+    slot_ref[...] = spots
+
     barrier = pltpu.get_barrier_semaphore()
 
     def greet(target):
@@ -136,9 +152,9 @@
     HALF = GROUP // 2
 
     def z_part(kind, way, hop, sub):
-        near, far = ((kn, kf), (vn, vf))[kind]
-        at = ((0, 4, 3, 2, 1), (0, 1, 2, 0, 1))[way][hop] * GROUP + sub * HALF
-        return (near if hop <= 2 else far).at[pl.ds(at, HALF)]
+        bufs = ((kn, km, kf), (vn, vm, vf))[kind]
+        at = ((0, 4, 3, 1, 0), (0, 1, 2, 0, 0))[way][hop] * GROUP + sub * HALF
+        return bufs[max(hop - 2, 0)].at[pl.ds(at, HALF)]
 
     def z_copy(kind, way, step, sub):
         target = dev(x, y, (z + 1) % NZ if way == 0 else (z + 7) % NZ, c)
@@ -160,16 +176,16 @@
 
     up = dev_ab(a, (b + 1) % 4, z, c)
     down = dev_ab(a, (b + 3) % 4, z, c)
-    total_u = U[0] + U[1]
 
     def b_copy(kind, part, n):
         have = (ku, vu)[kind]
         rel = (krl, vrl)[kind]
+        pack = (kpack, vpack)[kind]
         u = U[part]
         h = u // 2
-        p = 3 * U[0] * part
+        p = 3 * OFF[part]
         f = HELD + p
-        l = U[0] * part
+        l = OFF[part]
         src, dst, target = (
             (pack.at[pl.ds(p, u)], have.at[pl.ds(f, u)], up),
             (pack.at[pl.ds(p + 2 * u, u)], have.at[pl.ds(f + 2 * u, u)], down),
@@ -181,14 +197,18 @@
         return remote(src, dst, b_send.at[kind, part, n], b_recv.at[kind, part, n], target)
 
     def b_begin(kind, part):
-        held = ((kn, kf), (vn, vf))[kind][part]
+        bufs = ((kn, km, kf), (vn, vm, vf))[kind]
+        pack = (kpack, vpack)[kind]
         u = U[part]
-        p = 3 * U[0] * part
-        base, size = (0, NEAR) if part == 0 else (NEAR, AFAR)
 
         def one(r, _):
             for j in range(3):
-                pack[p + j * u + r] = held[jnp.clip(smem[2, (j + 1) * TW + U[0] * part + r] - base, 0, size - 1)]
+                i = smem[2, (j + 1) * TW + OFF[part] + r]
+                block = None
+                for k in range(part + 1):
+                    other = bufs[k][jnp.clip(i - STARTS[k], 0, CLASSES[k] - 1)]
+                    block = other if k == 0 else lax.select(i >= STARTS[k], other, block)
+                pack[3 * OFF[part] + j * u + r] = block
             return 0
 
         lax.fori_loop(0, u, one, 0)
@@ -205,18 +225,26 @@
             b_copy(kind, part, n).wait_recv()
 
     def keep(kind, part):
-        held = ((kn, kf), (vn, vf))[kind][part]
-        at = pl.ds(0, NEAR) if part == 0 else pl.ds(NEAR, AFAR)
-        return pltpu.make_async_copy(held, (ku, vu)[kind].at[at], loc.at[9 + 2 * kind + part])
+        held = ((kn, km, kf), (vn, vm, vf))[kind][part]
+        at = pl.ds(STARTS[part], CLASSES[part])
+        return pltpu.make_async_copy(held, (ku, vu)[kind].at[at], loc.at[9 + 3 * kind + part])
+
+    def keep_all(kind):
+        for part in range(3):
+            keep(kind, part).start()
+
+    def kept(kind):
+        for part in range(3):
+            keep(kind, part).wait()
 
     def b_sent(kind):
-        for part in range(2):
+        for part in range(3):
             for n in range(6):
                 b_copy(kind, part, n).wait_send()
 
-    def near_far(t):
-        far = (t // 32 - z + NZ) % NZ
-        return (far >= 3) & (far <= 5)
+    def distance_class(t):
+        off = (t // 32 - z + NZ) % NZ
+        return jnp.where(off == 4, 2, jnp.where((off == 3) | (off == 5), 1, 0))
 
     def lists():
         f32, bf16, i32 = jnp.float32, jnp.bfloat16, jnp.int32
@@ -238,18 +266,25 @@
         want = jnp.concatenate([by_y, by_x], axis=0)
         t0 = lax.broadcasted_iota(i32, (n, n), 0)
         t1 = lax.broadcasted_iota(i32, (n, n), 1)
-        before = (t0 < t1) & (near_far(t0) == near_far(t1))
+        class0, class1 = distance_class(t0), distance_class(t1)
+        before = (class0 < class1) | ((class0 == class1) & (t0 < t1))
         same_y = (t0 // 8) % NY == (t1 // 8) % NY
         same_x = t0 % NX == t1 % NX
-        rank_y = jnp.dot(want.astype(bf16), one(before & same_y).astype(bf16), preferred_element_type=f32)
-        rank_x = jnp.dot(want.astype(bf16), one(before & same_x).astype(bf16), preferred_element_type=f32)
+        want_b = want.astype(bf16)
+
+        def count(which):
+            return jnp.dot(want_b, one(which).astype(bf16), preferred_element_type=f32)
+
         group = lax.broadcasted_iota(i32, (8, n), 0)
         t8 = lax.broadcasted_iota(i32, (8, n), 1)
         first = group < 4
-        rank = jnp.where(first, rank_y, rank_x)
+        rank = jnp.where(first, count(before & same_y), count(before & same_x))
+        n0, n1 = [jnp.where(first, count(same_y & (class0 == k)), count(same_x & (class0 == k))) for k in range(2)]
         away = jnp.where(first, (t8 // 8) % NY, t8 % NX) != group % 4
-        room = jnp.where(near_far(t8), U[1], U[0]).astype(f32)
-        over = one((want > 0.5) & away & (rank > room - 0.5))
+        class8 = distance_class(t8)
+        rank = jnp.where(class8 >= 1, rank + jnp.maximum(U[0] - n0, 0.0), rank)
+        rank = jnp.where(class8 == 2, rank + jnp.maximum(OFF[2] - n1 - jnp.maximum(n0, float(U[0])), 0.0), rank)
+        over = one((want > 0.5) & away & (rank > total_u - 0.5))
         flags[z] = jnp.broadcast_to(jnp.max(over), (8, D)).astype(i32)
         wants[0] = want
         wants[1] = rank
@@ -258,8 +293,8 @@
         ta = tx * (1 - c) + ty * c
         tb = ty * (1 - c) + tx * c
         off = (tz - z + NZ) % NZ
-        local = jnp.where(off <= 2, off, jnp.where(off >= 6, off - 3, off + 2)) * GROUP + 2 * ta + tc
-        late = near_far(t)
+        spot = jnp.where(off <= 2, off, jnp.where(off >= 6, off - 3, jnp.where(off == 4, 7, jnp.where(off == 3, 5, 6))))
+        local = spot * GROUP + 2 * ta + tc
 
         def row(d):
             at = pl.ds(4 * c + d, 1)
@@ -267,7 +302,8 @@
 
         _, rk = row(b)
         gap = (b - tb + 4) % 4 - 1
-        there = HELD + jnp.where(late, 3 * U[0] + gap * U[1], gap * U[0]) + rk
+        shift = jnp.where(rk >= OFF[2], 2 * OFF[2] + gap * U[2], jnp.where(rk >= U[0], 2 * U[0] + gap * U[1], gap * U[0]))
+        there = HELD + rk + shift
         at = jnp.clip(jnp.where(tb == b, local, there), 0, HELD + 3 * total_u - 1)
         r8 = lax.broadcasted_iota(i32, (8, n), 0)
         at8 = jnp.broadcast_to(at, (8, n))
@@ -277,7 +313,7 @@
         k = lax.broadcasted_iota(i32, (TW, n), 0)
         for j in range(4):
             wj, rj = row((b + j) % 4)
-            kk = jnp.where((wj > 0.5) & (tb == b), rj + jnp.where(late, U[0], 0), -1)
+            kk = jnp.where((wj > 0.5) & (tb == b), rj, -1)
             picks.append(one(kk == k))
         picks = jnp.concatenate(picks, axis=0).astype(bf16)
         names = jnp.broadcast_to(local, (8, n)).astype(f32).astype(bf16)
@@ -326,7 +362,7 @@
                 pbuf[m, at, e * ROWS : (e + 1) * ROWS] = (parts[e] * inv).astype(jnp.bfloat16)
             return 0
 
-        lax.fori_loop(0, GQ // 2, heads, 0)
+        lax.fori_loop(0, GQ // 2, heads, 0, unroll=2)
         return 0
 
     def columns(head):
@@ -364,7 +400,7 @@
             obuf[m, :, pl.ds(pl.multiple_of(first + D, D), D)] = o[ROWS:]
             return 0
 
-        lax.fori_loop(0, GQ // 2, heads, 0)
+        lax.fori_loop(0, GQ // 2, heads, 0, unroll=2)
         for k in range(2):
             @pl.when(n == k)
             def _():
@@ -416,43 +452,44 @@
     to_scalars().wait()
     b_begin(0, 0)
     z_hop(0, 3)
+    b_begin(0, 1)
+    b_relay(0, 0)
     wait_exchange(1)
     z_first(1)
-    b_relay(0, 0)
     z_hop(0, 4)
-    keep(0, 0).start()
-    keep(0, 1).start()
-    b_begin(0, 1)
+    b_begin(0, 2)
+    keep_all(0)
+    b_relay(0, 1)
     z_hop(1, 1)
-    b_relay(0, 1)
+    b_relay(0, 2)
     z_hop(1, 2)
+    b_begin(1, 0)
+    wait_exchange(2)
     b_end(0, 0)
-    wait_exchange(2)
-    keep(0, 0).wait()
-    keep(0, 1).wait()
     b_end(0, 1)
-    b_sent(0)
-    b_begin(1, 0)
+    kept(0)
+    b_end(0, 2)
     lax.fori_loop(0, 1, scores, 0)
     z_hop(1, 3)
+    b_begin(1, 1)
     b_relay(1, 0)
     lax.fori_loop(1, 3, scores, 0)
+    b_relay(1, 1)
     z_hop(1, 4)
-    keep(1, 0).start()
-    keep(1, 1).start()
-    b_begin(1, 1)
+    b_begin(1, 2)
+    keep_all(1)
     lax.fori_loop(3, 5, scores, 0)
-    b_relay(1, 1)
+    b_relay(1, 2)
     lax.fori_loop(5, 8, scores, 0)
     b_end(1, 0)
-    keep(1, 0).wait()
-    keep(1, 1).wait()
     b_end(1, 1)
+    kept(1)
+    b_end(1, 2)
     lax.fori_loop(0, 8, attend, 0)
 
     for n in range(1, 8):
         tz_copy(1, n, True).wait_recv()
-    flag_ref[...] = functools.reduce(jnp.maximum, [flags[i] for i in range(NZ)])
+    flag_ref[0, 0] = jnp.max(functools.reduce(jnp.maximum, [flags[i] for i in range(NZ)]))
     for n in range(1, 8):
         for copy in t_copy(n, False):
             copy.wait_send()
@@ -468,6 +505,7 @@
         for step in range(1, 5):
             for way, sub in z_parts(step):
                 z_copy(kind, way, step, sub).wait_send()
+    b_sent(0)
     b_sent(1)
     for k in range(2):
         out_via(k).wait_send()
@@ -488,29 +526,29 @@
             remote(dst, dst, o_send.at[0], o_recv.at[h], source).wait_recv()
 
 
-def attention(U, ident, named, slots, queries, keys, values):
+def attention(U, ident, selected, counts, slots, queries, keys, values):
     any_space = pl.BlockSpec(memory_space=pl.ANY)
-    vmem = pl.BlockSpec(memory_space=pltpu.VMEM)
+    smem = pl.BlockSpec(memory_space=pltpu.SMEM)
     block = (ROWS, D)
     bf16 = jnp.bfloat16
     dma = pltpu.SemaphoreType.DMA
-    near, far = U
+    total = sum(U)
     return pl.pallas_call(
         functools.partial(kernel, U),
-        out_shape=(jax.ShapeDtypeStruct(queries.shape, bf16), jax.ShapeDtypeStruct((8, D), jnp.int32)),
-        in_specs=[vmem] * 2 + [any_space] * 3,
-        out_specs=(any_space, vmem),
+        out_shape=(jax.ShapeDtypeStruct(queries.shape, bf16), jax.ShapeDtypeStruct((1, 1), jnp.int32)),
+        in_specs=[smem] * 3 + [any_space] * 3,
+        out_specs=(any_space, smem),
         scratch_shapes=[
+            pltpu.VMEM((4 * SEL, D), jnp.int32),
+            pltpu.VMEM((1, D), jnp.int32),
             pltpu.VMEM((GROUP, ROWS, GQ * D), bf16),
-            pltpu.VMEM((NEAR, *block), bf16),
-            pltpu.VMEM((AFAR, *block), bf16),
-            pltpu.VMEM((NEAR, *block), bf16),
-            pltpu.VMEM((AFAR, *block), bf16),
-            pltpu.VMEM((HELD + 3 * (near + far), *block), bf16),
-            pltpu.VMEM((HELD + 3 * (near + far), *block), bf16),
-            pltpu.VMEM((3 * (near + far), *block), bf16),
-            pltpu.VMEM((near + far, *block), bf16),
-            pltpu.VMEM((near + far, *block), bf16),
+            *[pltpu.VMEM((size, *block), bf16) for size in CLASSES * 2],
+            pltpu.VMEM((HELD + 3 * total, *block), bf16),
+            pltpu.VMEM((HELD + 3 * total, *block), bf16),
+            pltpu.VMEM((3 * total, *block), bf16),
+            pltpu.VMEM((3 * total, *block), bf16),
+            pltpu.VMEM((total, *block), bf16),
+            pltpu.VMEM((total, *block), bf16),
             pltpu.VMEM((SEL * ROWS, D), bf16),
             pltpu.VMEM((GROUP, GQ * ROWS, SEL * ROWS), bf16),
             pltpu.VMEM((GROUP, ROWS, GQ * D), bf16),
@@ -523,23 +561,20 @@
             pltpu.VMEM((NZ, 8, D), jnp.int32),
             dma((3, 8)), dma((3, 8)),
             dma((2, 2, 4, 2)), dma((2, 2, 4, 2)),
-            dma((2, 2, 6)), dma((2, 2, 6)),
+            dma((2, 3, 6)), dma((2, 3, 6)),
             dma((10,)), dma((8,)), dma((2,)),
             dma((4, 8)), dma((4, 8)),
-            dma((13,)),
+            dma((15,)),
         ],
         compiler_params=pltpu.CompilerParams(
             collective_id=ident, has_side_effects=True, vmem_limit_bytes=61 * 1024 * 1024),
-    )(named, slots, queries, keys, values)
+    )(selected, counts, slots, queries, keys, values)
 
 
 def body(queries, keys, values, selected, counts, block_slot):
-    live = jnp.arange(SEL, dtype=jnp.int32)[None, :] < counts[:, None]
-    named = jnp.where(live, (selected % NX) * (NZ * NY * 2) + selected // NX, -1)
-    named = jnp.broadcast_to(named.reshape(-1, 1), (4 * SEL, D))
-    slots = jnp.pad(block_slot, (0, D - 4))[None, :]
-    out, flag = attention(FAST, 0, named, slots, queries, keys, values)
-    again = lambda: attention(FULL, 1, named, slots, queries, keys, values)[0]
+    tables = (selected, counts, block_slot)
+    out, flag = attention(FAST, 0, *tables, queries, keys, values)
+    again = lambda: attention(FULL, 1, *tables, queries, keys, values)[0]
     return lax.cond(flag[0, 0] > 0, again, lambda: out)
 
 

time: 104 us -> 98 us (0.942)
  Pallas kernels: 97.6 us -> 93.8 us
  local copies, waits for them, and re-layouts: 5.25 us -> 3.12 us
    pallas_call x1, Pallas kernels: 97.6 us -> 93.8 us  [attention(): pl.pallas_call(functools.partial(kernel, U), out_shape=(jax.ShapeDtypeStr...]
    slice x1 -> x0, local copies, waits for them, and re-layouts: 1.18 us -> none  [body(): return lax.cond(flag[0, 0] > 0, again, lambda: out)]
    unnamed x7 -> x13, local copies, waits for them, and re-layouts: 3.11 us -> 3.12 us
where the time goes in v3:
time: 98 us; the launch traced here: 97.8 us
  Pallas kernels  93.8 us (96%)
  local copies, waits for them, and re-layouts  3.12 us (3%)
    pallas_call x1, Pallas kernels, attention(): pl.pallas_call(functools.partial(kernel, U), out_shape=(jax.ShapeDtypeStr...  93.8 us
    unnamed x13, local copies, waits for them, and re-layouts  3.12 us

profile of v3, /device:TPU:1, one launch (start us, length us, event | category | flops | bytes accessed | tf_op | source)
XLA Modules:
  0.0 97.8 jit_solution(7353588921296938703)
XLA Ops:
  0.0 0.0 copy-start.5
  0.0 0.0 copy-start.4
  0.0 0.0 copy-start.3
  0.0 0.0 copy-start.2
  0.0 0.0 copy-start.1
  0.0 0.0 copy-start
  0.0 93.8 %shard_map.66 = (bf16[128,8192]{1,0:T(8,128)(2,1)}, s32[1,1]{1,0:T(1,128)}) custom-call(s32[4,8]{1,0:T(4,128)} %sel_ref.1, s32[4]{0:T(128)} %count_ref.1, s32[4]{0:T(128)} %own_ref.1, bf16[128,8192]{1,0:T(8,128)(2,1)} %q_ref.1, bf16[128,1024]{1,0:T(8,128)(2,1)} %k_ref.1, bf16[128,1024]{1,0:T(8,128)(2,1)} %v_ref.1), custom_call_target="tpu_custom_call" | custom-call | tf_op jit(solution)/shard_map/pallas_call | solution.py:536
  94.4 0.0 copy-done.5
  94.4 0.0 copy-done.4
  94.5 0.0 copy-done.3
  94.5 0.0 copy-done.2
  94.5 0.0 copy-done.1
  94.5 0.0 copy-done
  94.5 0.2 conditional.1
  94.7 3.1 %copy.12 = bf16[128,8192]{1,0:T(8,128)(2,1)} copy(bf16[128,8192]{1,0:T(8,128)(2,1)} %get-tuple-element.32) | data formatting | bytes 4194304
Async XLA Ops:
  0.0 94.4 %copy-start.5 = (s32[4]{0:T(128)S(1)}, s32[4]{0:T(128)}, u32[]{:S(2)}) copy-start(s32[4]{0:T(128)} %own_ref.1) | copy-start | bytes 52
  0.0 94.4 %copy-start.4 = (s32[4]{0:T(128)S(1)}, s32[4]{0:T(128)}, u32[]{:S(2)}) copy-start(s32[4]{0:T(128)} %count_ref.1) | copy-start | bytes 52
  0.0 94.5 %copy-start.3 = (s32[4,8]{1,0:T(4,128)S(1)}, s32[4,8]{1,0:T(4,128)}, u32[]{:S(2)}) copy-start(s32[4,8]{1,0:T(4,128)} %sel_ref.1) | copy-start | bytes 388
  0.0 94.5 %copy-start.2 = (bf16[128,1024]{1,0:T(8,128)(2,1)S(1)}, bf16[128,1024]{1,0:T(8,128)(2,1)}, u32[]{:S(2)}) copy-start(bf16[128,1024]{1,0:T(8,128)(2,1)} %v_ref.1) | copy-start | bytes 786436
  0.0 94.5 %copy-start.1 = (bf16[128,1024]{1,0:T(8,128)(2,1)S(1)}, bf16[128,1024]{1,0:T(8,128)(2,1)}, u32[]{:S(2)}) copy-start(bf16[128,1024]{1,0:T(8,128)(2,1)} %k_ref.1) | copy-start | bytes 786436
  0.0 94.5 %copy-start = (bf16[128,8192]{1,0:T(8,128)(2,1)S(1)}, bf16[128,8192]{1,0:T(8,128)(2,1)}, u32[]{:S(2)}) copy-start(bf16[128,8192]{1,0:T(8,128)(2,1)} %q_ref.1) | copy-start | bytes 6291460

commit v4 on v3

--- a/solution.py
+++ b/solution.py
@@ -47,6 +47,8 @@
                                             device_id=target, device_id_type=MESH)
 
     OFF = (0, U[0], U[0] + U[1])
+    shared = U == FULL
+    packs = (kpack, kpack if shared else vpack)
     total_u = sum(U)
 
     row = lax.broadcasted_iota(jnp.int32, (4 * SEL, D), 0)
@@ -180,7 +182,7 @@
     def b_copy(kind, part, n):
         have = (ku, vu)[kind]
         rel = (krl, vrl)[kind]
-        pack = (kpack, vpack)[kind]
+        pack = packs[kind]
         u = U[part]
         h = u // 2
         p = 3 * OFF[part]
@@ -198,7 +200,7 @@
 
     def b_begin(kind, part):
         bufs = ((kn, km, kf), (vn, vm, vf))[kind]
-        pack = (kpack, vpack)[kind]
+        pack = packs[kind]
         u = U[part]
 
         def one(r, _):
@@ -387,8 +389,8 @@
 
     def attend(n, _):
         q = n // 2
-        i = jnp.where(q < 2, 2 + q, 3 - q)
-        cc = n % 2
+        i = jnp.where(q == 0, 2, jnp.where(q == 3, 0, 1 + 2 * (n % 2)))
+        cc = jnp.where((q == 0) | (q == 3), n % 2, q - 1)
         m = 2 * ((a + i) % 4) + cc
         gather_entries(vu, m)
 
@@ -405,19 +407,22 @@
             @pl.when(n == k)
             def _():
                 out_via(k).start()
-        for q0, i0 in ((1, 3), (2, 1), (3, 0)):
-            for k in range(2):
-                @pl.when((n == 2 * q0 + k) & ((i0 > 0) | (c != k)))
-                def _():
-                    out_copy(i0, k).start()
+        for k in range(4):
+            @pl.when(n == 2 + k)
+            def _():
+                out_copy(1 + 2 * (k % 2), k // 2).start()
+        for k in range(2):
+            @pl.when((n == 6 + k) & (c != k))
+            def _():
+                out_copy(0, k).start()
 
         @pl.when(n == 6 + c)
         def _():
             out_local().start()
 
-        @pl.when(n == 4)
-        def _():
-            for k in range(2):
+        for k in range(2):
+            @pl.when(n == 5 + k)
+            def _():
                 remote(orl.at[k], orl.at[k], o_send.at[4 + k], r_recv.at[k],
                        dev_ab((a + (3 if k == 0 else 1)) % 4, b, z, c)).wait_recv()
                 out_relay(k).start()
@@ -463,24 +468,26 @@
     z_hop(1, 1)
     b_relay(0, 2)
     z_hop(1, 2)
+    if shared:
+        b_sent(0)
     b_begin(1, 0)
     wait_exchange(2)
     b_end(0, 0)
     b_end(0, 1)
     kept(0)
     b_end(0, 2)
-    lax.fori_loop(0, 1, scores, 0)
+    lax.fori_loop(0, 2, scores, 0)
     z_hop(1, 3)
     b_begin(1, 1)
     b_relay(1, 0)
-    lax.fori_loop(1, 3, scores, 0)
-    b_relay(1, 1)
+    lax.fori_loop(2, 4, scores, 0)
     z_hop(1, 4)
     b_begin(1, 2)
     keep_all(1)
-    lax.fori_loop(3, 5, scores, 0)
+    b_relay(1, 1)
+    lax.fori_loop(4, 6, scores, 0)
     b_relay(1, 2)
-    lax.fori_loop(5, 8, scores, 0)
+    lax.fori_loop(6, 8, scores, 0)
     b_end(1, 0)
     b_end(1, 1)
     kept(1)
@@ -505,7 +512,8 @@
         for step in range(1, 5):
             for way, sub in z_parts(step):
                 z_copy(kind, way, step, sub).wait_send()
-    b_sent(0)
+    if not shared:
+        b_sent(0)
     b_sent(1)
     for k in range(2):
         out_via(k).wait_send()
@@ -535,9 +543,9 @@
     total = sum(U)
     return pl.pallas_call(
         functools.partial(kernel, U),
-        out_shape=(jax.ShapeDtypeStruct(queries.shape, bf16), jax.ShapeDtypeStruct((1, 1), jnp.int32)),
+        out_shape=(pltpu.VMEM(queries.shape, bf16), jax.ShapeDtypeStruct((1, 1), jnp.int32)),
         in_specs=[smem] * 3 + [any_space] * 3,
-        out_specs=(any_space, smem),
+        out_specs=(pl.BlockSpec(memory_space=pltpu.VMEM), smem),
         scratch_shapes=[
             pltpu.VMEM((4 * SEL, D), jnp.int32),
             pltpu.VMEM((1, D), jnp.int32),
@@ -546,7 +554,7 @@
             pltpu.VMEM((HELD + 3 * total, *block), bf16),
             pltpu.VMEM((HELD + 3 * total, *block), bf16),
             pltpu.VMEM((3 * total, *block), bf16),
-            pltpu.VMEM((3 * total, *block), bf16),
+            pltpu.VMEM((1 if U == FULL else 3 * total, *block), bf16),
             pltpu.VMEM((total, *block), bf16),
             pltpu.VMEM((total, *block), bf16),
             pltpu.VMEM((SEL * ROWS, D), bf16),
@@ -567,7 +575,7 @@
             dma((15,)),
         ],
         compiler_params=pltpu.CompilerParams(
-            collective_id=ident, has_side_effects=True, vmem_limit_bytes=61 * 1024 * 1024),
+            collective_id=ident, has_side_effects=True, vmem_limit_bytes=(58 if U == FULL else 44) * 1024 * 1024),
     )(selected, counts, slots, queries, keys, values)
 
 

time: 98 us -> 93.8 us (0.957)
  Pallas kernels: 93.8 us -> 91.4 us
  local copies, waits for them, and re-layouts: 3.12 us -> 1.35 us
    pallas_call x1, Pallas kernels: 93.8 us -> 91.4 us  [attention(): pl.pallas_call(functools.partial(kernel, U), out_shape=(pltpu.VMEM(querie...]
    unnamed x13, local copies, waits for them, and re-layouts: 3.12 us -> 1.35 us
where the time goes in v4:
time: 93.8 us; the launch traced here: 93.7 us
  Pallas kernels  91.4 us (97%)
  local copies, waits for them, and re-layouts  1.35 us (1%)
    pallas_call x1, Pallas kernels, attention(): pl.pallas_call(functools.partial(kernel, U), out_shape=(pltpu.VMEM(querie...  91.4 us

profile of v4, /device:TPU:1, one launch (start us, length us, event | category | flops | bytes accessed | tf_op | source)
XLA Modules:
  0.0 93.7 jit_solution(15499678220511121731)
XLA Ops:
  0.0 0.0 copy-start.5
  0.0 0.0 copy-start.4
  0.0 0.0 copy-start.3
  0.0 0.0 copy-start.2
  0.0 0.0 copy-start.1
  0.0 0.0 copy-start
  0.0 91.4 %shard_map.66 = (bf16[128,8192]{1,0:T(8,128)(2,1)S(1)}, s32[1,1]{1,0:T(1,128)}) custom-call(s32[4,8]{1,0:T(4,128)} %sel_ref.1, s32[4]{0:T(128)} %count_ref.1, s32[4]{0:T(128)} %own_ref.1, bf16[128,8192]{1,0:T(8,128)(2,1)} %q_ref.1, bf16[128,1024]{1,0:T(8,128)(2,1)} %k_ref.1, bf16[128,1024]{1,0:T(8,128)(2,1)} %v_ref.1), custom_call_target="tpu_custom_call" | custom-call | tf_op jit(solution)/shard_map/pallas_call | solution.py:544
  92.0 0.0 copy-done.5
  92.1 0.0 copy-done.4
  92.1 0.0 copy-done.3
  92.1 0.0 copy-done.2
  92.1 0.0 copy-done.1
  92.1 0.0 copy-done
  92.1 0.2 conditional.1
  92.3 1.3 %copy.12 = bf16[128,8192]{1,0:T(8,128)(2,1)} copy(bf16[128,8192]{1,0:T(8,128)(2,1)S(1)} %get-tuple-element.32) | data formatting | bytes 4194304
Async XLA Ops:
  0.0 92.0 %copy-start.5 = (s32[4]{0:T(128)S(1)}, s32[4]{0:T(128)}, u32[]{:S(2)}) copy-start(s32[4]{0:T(128)} %own_ref.1) | copy-start | bytes 52
  0.0 92.1 %copy-start.4 = (s32[4]{0:T(128)S(1)}, s32[4]{0:T(128)}, u32[]{:S(2)}) copy-start(s32[4]{0:T(128)} %count_ref.1) | copy-start | bytes 52
  0.0 92.1 %copy-start.3 = (s32[4,8]{1,0:T(4,128)S(1)}, s32[4,8]{1,0:T(4,128)}, u32[]{:S(2)}) copy-start(s32[4,8]{1,0:T(4,128)} %sel_ref.1) | copy-start | bytes 388
  0.0 92.1 %copy-start.2 = (bf16[128,1024]{1,0:T(8,128)(2,1)S(1)}, bf16[128,1024]{1,0:T(8,128)(2,1)}, u32[]{:S(2)}) copy-start(bf16[128,1024]{1,0:T(8,128)(2,1)} %v_ref.1) | copy-start | bytes 786436
  0.0 92.1 %copy-start.1 = (bf16[128,1024]{1,0:T(8,128)(2,1)S(1)}, bf16[128,1024]{1,0:T(8,128)(2,1)}, u32[]{:S(2)}) copy-start(bf16[128,1024]{1,0:T(8,128)(2,1)} %k_ref.1) | copy-start | bytes 786436
  0.0 92.1 %copy-start = (bf16[128,8192]{1,0:T(8,128)(2,1)S(1)}, bf16[128,8192]{1,0:T(8,128)(2,1)}, u32[]{:S(2)}) copy-start(bf16[128,8192]{1,0:T(8,128)(2,1)} %q_ref.1) | copy-start | bytes 6291460

commit v5 on v4

--- a/solution.py
+++ b/solution.py
@@ -134,7 +134,7 @@
     def exchange(kind):
         each_piece(kind, send_piece, lambda kind, t: local_piece(kind, t).start())
 
-    def wait_exchange(kind):
+    def wait_exchange(kind, places=(0, 1, 3, 2)):
         _, dst, _ = kinds[kind]
 
         def one(i, cc):
@@ -142,21 +142,21 @@
             slot = 2 * aa + cc
             remote(dst.at[slot], dst.at[slot], ex_send.at[kind, 0], ex_recv.at[kind, slot], dev_ab(aa, b, z, cc)).wait_recv()
 
-        for i in range(1, 4):
-            for cc in range(2):
-                one(i, cc)
-        one(0, 1 - c)
-        for t in range(2):
-            @pl.when(c == t)
-            def _():
-                local_piece(kind, t).wait()
-
-    HALF = GROUP // 2
+        for i in places:
+            if i:
+                for cc in range(2):
+                    one(i, cc)
+            else:
+                one(0, 1 - c)
+                for t in range(2):
+                    @pl.when(c == t)
+                    def _():
+                        local_piece(kind, t).wait()
 
     def z_part(kind, way, hop, sub):
         bufs = ((kn, km, kf), (vn, vm, vf))[kind]
-        at = ((0, 4, 3, 1, 0), (0, 1, 2, 0, 0))[way][hop] * GROUP + sub * HALF
-        return bufs[max(hop - 2, 0)].at[pl.ds(at, HALF)]
+        at = ((0, 4, 3, 1, 0), (0, 1, 2, 0, 0))[way][hop] * GROUP + 2 * ((a + sub) % 4)
+        return bufs[max(hop - 2, 0)].at[pl.ds(at, 2)]
 
     def z_copy(kind, way, step, sub):
         target = dev(x, y, (z + 1) % NZ if way == 0 else (z + 7) % NZ, c)
@@ -164,11 +164,13 @@
                       z_send.at[kind, way, step - 1, sub], z_recv.at[kind, way, step - 1, sub], target)
 
     def z_parts(step):
-        return [(way, sub) for sub in range(2) for way in range(2) if step < 4 or way == sub]
+        return [(way, sub) for sub in (0, 1, 3, 2) for way in range(2) if step < 4 or way == sub // 2]
 
     def z_first(kind):
-        for way, sub in z_parts(1):
-            z_copy(kind, way, 1, sub).start()
+        for sub in (0, 1, 3, 2):
+            wait_exchange(kind, (sub,))
+            for way in range(2):
+                z_copy(kind, way, 1, sub).start()
 
     def z_hop(kind, step):
         for way, sub in z_parts(step):
@@ -436,9 +438,8 @@
     for copy in t_local():
         copy.start()
     exchange(1)
+    z_first(0)
     exchange(2)
-    wait_exchange(0)
-    z_first(0)
     for n in range(1, 8):
         for copy in t_copy(n, True):
             copy.wait_recv()
@@ -447,10 +448,10 @@
     for n in range(1, 8):
         tz_copy(0, n, False).start()
     z_hop(0, 1)
+    z_hop(0, 2)
     for n in range(1, 8):
         tz_copy(0, n, True).wait_recv()
     lists()
-    z_hop(0, 2)
     to_scalars().start()
     for n in range(1, 8):
         tz_copy(1, n, False).start()
@@ -459,7 +460,6 @@
     z_hop(0, 3)
     b_begin(0, 1)
     b_relay(0, 0)
-    wait_exchange(1)
     z_first(1)
     z_hop(0, 4)
     b_begin(0, 2)
@@ -568,7 +568,7 @@
             pltpu.SMEM((8, 256), jnp.int32),
             pltpu.VMEM((NZ, 8, D), jnp.int32),
             dma((3, 8)), dma((3, 8)),
-            dma((2, 2, 4, 2)), dma((2, 2, 4, 2)),
+            dma((2, 2, 4, 4)), dma((2, 2, 4, 4)),
             dma((2, 3, 6)), dma((2, 3, 6)),
             dma((10,)), dma((8,)), dma((2,)),
             dma((4, 8)), dma((4, 8)),

time: 93.8 us -> 91.4 us (0.974)
  Pallas kernels: 91.4 us -> 88.9 us
    pallas_call x1, Pallas kernels: 91.4 us -> 88.9 us  [attention(): pl.pallas_call(functools.partial(kernel, U), out_shape=(pltpu.VMEM(querie...]
where the time goes in v5:
time: 91.4 us; the launch traced here: 91.2 us
  Pallas kernels  88.9 us (97%)
  local copies, waits for them, and re-layouts  1.35 us (1%)
    pallas_call x1, Pallas kernels, attention(): pl.pallas_call(functools.partial(kernel, U), out_shape=(pltpu.VMEM(querie...  88.9 us

profile of v5, /device:TPU:1, one launch (start us, length us, event | category | flops | bytes accessed | tf_op | source)
XLA Modules:
  0.0 91.2 jit_solution(8286098305462284892)
XLA Ops:
  0.0 0.0 copy-start.5
  0.0 0.0 copy-start.4
  0.0 0.0 copy-start.3
  0.0 0.0 copy-start.2
  0.0 0.0 copy-start.1
  0.0 0.0 copy-start
  0.0 88.9 %shard_map.66 = (bf16[128,8192]{1,0:T(8,128)(2,1)S(1)}, s32[1,1]{1,0:T(1,128)}) custom-call(s32[4,8]{1,0:T(4,128)} %sel_ref.1, s32[4]{0:T(128)} %count_ref.1, s32[4]{0:T(128)} %own_ref.1, bf16[128,8192]{1,0:T(8,128)(2,1)} %q_ref.1, bf16[128,1024]{1,0:T(8,128)(2,1)} %k_ref.1, bf16[128,1024]{1,0:T(8,128)(2,1)} %v_ref.1), custom_call_target="tpu_custom_call" | custom-call | tf_op jit(solution)/shard_map/pallas_call | solution.py:544
  89.6 0.0 copy-done.5
  89.6 0.0 copy-done.4
  89.6 0.0 copy-done.3
  89.6 0.0 copy-done.2
  89.7 0.0 copy-done.1
  89.7 0.0 copy-done
  89.7 0.2 conditional.1
  89.9 1.3 %copy.12 = bf16[128,8192]{1,0:T(8,128)(2,1)} copy(bf16[128,8192]{1,0:T(8,128)(2,1)S(1)} %get-tuple-element.32) | data formatting | bytes 4194304
Async XLA Ops:
  0.0 89.6 %copy-start.5 = (s32[4]{0:T(128)S(1)}, s32[4]{0:T(128)}, u32[]{:S(2)}) copy-start(s32[4]{0:T(128)} %own_ref.1) | copy-start | bytes 52
  0.0 89.6 %copy-start.4 = (s32[4]{0:T(128)S(1)}, s32[4]{0:T(128)}, u32[]{:S(2)}) copy-start(s32[4]{0:T(128)} %count_ref.1) | copy-start | bytes 52
  0.0 89.6 %copy-start.3 = (s32[4,8]{1,0:T(4,128)S(1)}, s32[4,8]{1,0:T(4,128)}, u32[]{:S(2)}) copy-start(s32[4,8]{1,0:T(4,128)} %sel_ref.1) | copy-start | bytes 388
  0.0 89.6 %copy-start.2 = (bf16[128,1024]{1,0:T(8,128)(2,1)S(1)}, bf16[128,1024]{1,0:T(8,128)(2,1)}, u32[]{:S(2)}) copy-start(bf16[128,1024]{1,0:T(8,128)(2,1)} %v_ref.1) | copy-start | bytes 786436
  0.0 89.6 %copy-start.1 = (bf16[128,1024]{1,0:T(8,128)(2,1)S(1)}, bf16[128,1024]{1,0:T(8,128)(2,1)}, u32[]{:S(2)}) copy-start(bf16[128,1024]{1,0:T(8,128)(2,1)} %k_ref.1) | copy-start | bytes 786436
  0.0 89.6 %copy-start = (bf16[128,8192]{1,0:T(8,128)(2,1)S(1)}, bf16[128,8192]{1,0:T(8,128)(2,1)}, u32[]{:S(2)}) copy-start(bf16[128,8192]{1,0:T(8,128)(2,1)} %q_ref.1) | copy-start | bytes 6291460

commit v6 on v5

--- a/solution.py
+++ b/solution.py
@@ -372,19 +372,33 @@
     def columns(head):
         return out_ref.at[:, pl.ds(pl.multiple_of(head * GQ * D, GQ * D), GQ * D)]
 
-    def out_copy(i, cc):
+    WIDE = GQ * D // 2
+
+    def half_columns(head, half):
+        return out_ref.at[:, pl.ds(pl.multiple_of(head * GQ * D + half * WIDE, WIDE), WIDE)]
+
+    def out_half(m, half):
+        return obuf.at[m, :, pl.ds(half * WIDE, WIDE)]
+
+    def relay_half(cc, half):
+        return orl.at[cc, :, pl.ds(half * WIDE, WIDE)]
+
+    def out_copy(i, cc, half):
         m = 2 * ((a + i) % 4) + cc
-        return remote(obuf.at[m], columns(g), o_send.at[2 * i + cc], o_recv.at[g], dev_ab((a + i) % 4, b, z, cc))
-
-    def out_via(cc):
+        return remote(out_half(m, half), half_columns(g, half), o_send.at[2 * i + cc, half], o_recv.at[g, half],
+                      dev_ab((a + i) % 4, b, z, cc))
+
+    def out_via(cc, half):
         m = 2 * ((a + 2) % 4) + cc
         step = 1 if cc == 0 else 3
-        return remote(obuf.at[m], orl.at[cc], o_send.at[4 + cc], r_recv.at[cc], dev_ab((a + step) % 4, b, z, c))
-
-    def out_relay(cc):
+        return remote(out_half(m, half), relay_half(cc, half), o_send.at[4 + cc, half], r_recv.at[cc, half],
+                      dev_ab((a + step) % 4, b, z, c))
+
+    def out_relay(cc, half):
         step = 1 if cc == 0 else 3
         source = (a + 4 - step) % 4 + 4 * c
-        return remote(orl.at[cc], columns(source), o_send.at[8 + cc], o_recv.at[source], dev_ab((a + step) % 4, b, z, cc))
+        return remote(relay_half(cc, half), half_columns(source, half), o_send.at[8 + cc, half], o_recv.at[source, half],
+                      dev_ab((a + step) % 4, b, z, cc))
 
     def out_local():
         return pltpu.make_async_copy(obuf.at[2 * a + c], columns(g), loc.at[5])
@@ -404,19 +418,20 @@
             obuf[m, :, pl.ds(pl.multiple_of(first + D, D), D)] = o[ROWS:]
             return 0
 
-        lax.fori_loop(0, GQ // 2, heads, 0, unroll=2)
-        for k in range(2):
-            @pl.when(n == k)
-            def _():
-                out_via(k).start()
-        for k in range(4):
-            @pl.when(n == 2 + k)
-            def _():
-                out_copy(1 + 2 * (k % 2), k // 2).start()
-        for k in range(2):
-            @pl.when((n == 6 + k) & (c != k))
-            def _():
-                out_copy(0, k).start()
+        for half in range(2):
+            lax.fori_loop(2 * half, 2 * half + 2, heads, 0, unroll=2)
+            for k in range(2):
+                @pl.when(n == k)
+                def _():
+                    out_via(k, half).start()
+            for k in range(4):
+                @pl.when(n == 2 + k)
+                def _():
+                    out_copy(1 + 2 * (k % 2), k // 2, half).start()
+            for k in range(2):
+                @pl.when((n == 6 + k) & (c != k))
+                def _():
+                    out_copy(0, k, half).start()
 
         @pl.when(n == 6 + c)
         def _():
@@ -425,9 +440,11 @@
         for k in range(2):
             @pl.when(n == 5 + k)
             def _():
-                remote(orl.at[k], orl.at[k], o_send.at[4 + k], r_recv.at[k],
-                       dev_ab((a + (3 if k == 0 else 1)) % 4, b, z, c)).wait_recv()
-                out_relay(k).start()
+                for half in range(2):
+                    here = relay_half(k, half)
+                    remote(here, here, o_send.at[4 + k, half], r_recv.at[k, half],
+                           dev_ab((a + (3 if k == 0 else 1)) % 4, b, z, c)).wait_recv()
+                    out_relay(k, half).start()
 
         return 0
 
@@ -516,22 +533,24 @@
         b_sent(0)
     b_sent(1)
     for k in range(2):
-        out_via(k).wait_send()
-        out_relay(k).wait_send()
-        for i in (1, 3):
-            out_copy(i, k).wait_send()
-
-        @pl.when(c != k)
-        def _():
-            out_copy(0, k).wait_send()
+        for half in range(2):
+            out_via(k, half).wait_send()
+            out_relay(k, half).wait_send()
+            for i in (1, 3):
+                out_copy(i, k, half).wait_send()
+
+            @pl.when(c != k)
+            def _():
+                out_copy(0, k, half).wait_send()
     out_local().wait()
     for h in range(8):
-        dst = out_ref.at[:, pl.ds(h * GQ * D, GQ * D)]
         source = dev(h % 4, y, z, 0) if h < 4 else dev(x, h % 4, z, 1)
 
         @pl.when(g != h)
         def _():
-            remote(dst, dst, o_send.at[0], o_recv.at[h], source).wait_recv()
+            for half in range(2):
+                dst = half_columns(h, half)
+                remote(dst, dst, o_send.at[0, half], o_recv.at[h, half], source).wait_recv()
 
 
 def attention(U, ident, selected, counts, slots, queries, keys, values):
@@ -570,7 +589,7 @@
             dma((3, 8)), dma((3, 8)),
             dma((2, 2, 4, 4)), dma((2, 2, 4, 4)),
             dma((2, 3, 6)), dma((2, 3, 6)),
-            dma((10,)), dma((8,)), dma((2,)),
+            dma((10, 2)), dma((8, 2)), dma((2, 2)),
             dma((4, 8)), dma((4, 8)),
             dma((15,)),
         ],

time: 91.4 us -> 91.2 us (level)
  no operation moved by 1% of the time
where the time goes in v6:
time: 91.2 us; the launch traced here: 91 us
  Pallas kernels  88.7 us (97%)
  local copies, waits for them, and re-layouts  1.35 us (1%)
    pallas_call x1, Pallas kernels, attention(): pl.pallas_call(functools.partial(kernel, U), out_shape=(pltpu.VMEM(querie...  88.7 us

profile of v6, /device:TPU:1, one launch (start us, length us, event | category | flops | bytes accessed | tf_op | source)
XLA Modules:
  0.0 91.0 jit_solution(5070346927995200003)
XLA Ops:
  0.0 0.0 copy-start.5
  0.0 0.0 copy-start.4
  0.0 0.0 copy-start.3
  0.0 0.0 copy-start.2
  0.0 0.0 copy-start.1
  0.0 0.0 copy-start
  0.0 88.7 %shard_map.66 = (bf16[128,8192]{1,0:T(8,128)(2,1)S(1)}, s32[1,1]{1,0:T(1,128)}) custom-call(s32[4,8]{1,0:T(4,128)} %sel_ref.1, s32[4]{0:T(128)} %count_ref.1, s32[4]{0:T(128)} %own_ref.1, bf16[128,8192]{1,0:T(8,128)(2,1)} %q_ref.1, bf16[128,1024]{1,0:T(8,128)(2,1)} %k_ref.1, bf16[128,1024]{1,0:T(8,128)(2,1)} %v_ref.1), custom_call_target="tpu_custom_call" | custom-call | tf_op jit(solution)/shard_map/pallas_call | solution.py:563
  89.4 0.0 copy-done.5
  89.4 0.0 copy-done.4
  89.4 0.0 copy-done.3
  89.4 0.0 copy-done.2
  89.4 0.0 copy-done.1
  89.4 0.0 copy-done
  89.4 0.2 conditional.1
  89.7 1.3 %copy.12 = bf16[128,8192]{1,0:T(8,128)(2,1)} copy(bf16[128,8192]{1,0:T(8,128)(2,1)S(1)} %get-tuple-element.32) | data formatting | bytes 4194304
Async XLA Ops:
  0.0 89.4 %copy-start.5 = (s32[4]{0:T(128)S(1)}, s32[4]{0:T(128)}, u32[]{:S(2)}) copy-start(s32[4]{0:T(128)} %own_ref.1) | copy-start | bytes 52
  0.0 89.4 %copy-start.4 = (s32[4]{0:T(128)S(1)}, s32[4]{0:T(128)}, u32[]{:S(2)}) copy-start(s32[4]{0:T(128)} %count_ref.1) | copy-start | bytes 52
  0.0 89.4 %copy-start.3 = (s32[4,8]{1,0:T(4,128)S(1)}, s32[4,8]{1,0:T(4,128)}, u32[]{:S(2)}) copy-start(s32[4,8]{1,0:T(4,128)} %sel_ref.1) | copy-start | bytes 388
  0.0 89.4 %copy-start.2 = (bf16[128,1024]{1,0:T(8,128)(2,1)S(1)}, bf16[128,1024]{1,0:T(8,128)(2,1)}, u32[]{:S(2)}) copy-start(bf16[128,1024]{1,0:T(8,128)(2,1)} %v_ref.1) | copy-start | bytes 786436
  0.0 89.4 %copy-start.1 = (bf16[128,1024]{1,0:T(8,128)(2,1)S(1)}, bf16[128,1024]{1,0:T(8,128)(2,1)}, u32[]{:S(2)}) copy-start(bf16[128,1024]{1,0:T(8,128)(2,1)} %k_ref.1) | copy-start | bytes 786436
  0.0 89.4 %copy-start = (bf16[128,8192]{1,0:T(8,128)(2,1)S(1)}, bf16[128,8192]{1,0:T(8,128)(2,1)}, u32[]{:S(2)}) copy-start(bf16[128,8192]{1,0:T(8,128)(2,1)} %q_ref.1) | copy-start | bytes 6291460

commit v7 on v5

--- a/solution.py
+++ b/solution.py
@@ -24,7 +24,7 @@
 
 
 def kernel(U, sel_ref, count_ref, own_ref, q_ref, k_ref, v_ref, out_ref, flag_ref,
-           key_ref, slot_ref, qbuf, kn, km, kf, vn, vm, vf, ku, vu, kpack, vpack, krl, vrl, cat, pbuf, obuf, orl, keyt, slott, wants, index, smem, flags,
+           key_ref, slot_ref, kin, qbuf, kn, km, kf, vn, vm, vf, ku, vu, kpack, vpack, krl, vrl, cat, pbuf, obuf, orl, keyt, slott, wants, index, smem, flags,
            ex_send, ex_recv, z_send, z_recv, b_send, b_recv, o_send, o_recv, r_recv, t_send, t_recv, loc):
     s = lax.axis_index("seq")
     x = lax.axis_index("head")
@@ -50,6 +50,9 @@
     shared = U == FULL
     packs = (kpack, kpack if shared else vpack)
     total_u = sum(U)
+
+    to_kin = pltpu.make_async_copy(k_ref, kin, loc.at[15])
+    to_kin.start()
 
     row = lax.broadcasted_iota(jnp.int32, (4 * SEL, D), 0)
     lane = lax.broadcasted_iota(jnp.int32, (1, D), 1)
@@ -99,7 +102,7 @@
         return (pltpu.make_async_copy(key_ref, keyt.at[r0], loc.at[6]),
                 pltpu.make_async_copy(slot_ref, slott.at[z, pl.ds(r0, 1)], loc.at[7]))
 
-    kinds = ((k_ref, kn, D), (v_ref, vn, D), (q_ref, qbuf, GQ * D))
+    kinds = ((kin, kn, D), (v_ref, vn, D), (q_ref, qbuf, GQ * D))
 
     def piece(kind, t, i):
         src, dst, width = kinds[kind]
@@ -431,6 +434,7 @@
 
         return 0
 
+    to_kin.wait()
     exchange(0)
     for n in range(1, 8):
         for copy in t_copy(n, False):
@@ -549,6 +553,7 @@
         scratch_shapes=[
             pltpu.VMEM((4 * SEL, D), jnp.int32),
             pltpu.VMEM((1, D), jnp.int32),
+            pltpu.VMEM(keys.shape, bf16),
             pltpu.VMEM((GROUP, ROWS, GQ * D), bf16),
             *[pltpu.VMEM((size, *block), bf16) for size in CLASSES * 2],
             pltpu.VMEM((HELD + 3 * total, *block), bf16),
@@ -572,7 +577,7 @@
             dma((2, 3, 6)), dma((2, 3, 6)),
             dma((10,)), dma((8,)), dma((2,)),
             dma((4, 8)), dma((4, 8)),
-            dma((15,)),
+            dma((16,)),
         ],
         compiler_params=pltpu.CompilerParams(
             collective_id=ident, has_side_effects=True, vmem_limit_bytes=(58 if U == FULL else 44) * 1024 * 1024),

time: 91.4 us -> 91.1 us (level)
  no operation moved by 1% of the time
where the time goes in v7:
time: 91.1 us; the launch traced here: 91 us
  Pallas kernels  88.7 us (97%)
  local copies, waits for them, and re-layouts  1.35 us (1%)
    pallas_call x1, Pallas kernels, attention(): pl.pallas_call(functools.partial(kernel, U), out_shape=(pltpu.VMEM(querie...  88.7 us

profile of v7, /device:TPU:1, one launch (start us, length us, event | category | flops | bytes accessed | tf_op | source)
XLA Modules:
  0.0 91.0 jit_solution(14681016753866164545)
XLA Ops:
  0.0 0.0 copy-start.5
  0.0 0.0 copy-start.4
  0.0 0.0 copy-start.3
  0.0 0.0 copy-start.2
  0.0 0.0 copy-start.1
  0.0 0.0 copy-start
  0.0 88.7 %shard_map.66 = (bf16[128,8192]{1,0:T(8,128)(2,1)S(1)}, s32[1,1]{1,0:T(1,128)}) custom-call(s32[4,8]{1,0:T(4,128)} %sel_ref.1, s32[4]{0:T(128)} %count_ref.1, s32[4]{0:T(128)} %own_ref.1, bf16[128,8192]{1,0:T(8,128)(2,1)} %q_ref.1, bf16[128,1024]{1,0:T(8,128)(2,1)} %k_ref.1, bf16[128,1024]{1,0:T(8,128)(2,1)} %v_ref.1), custom_call_target="tpu_custom_call" | custom-call | tf_op jit(solution)/shard_map/pallas_call | solution.py:548
  89.4 0.0 copy-done.5
  89.4 0.0 copy-done.4
  89.4 0.0 copy-done.3
  89.5 0.0 copy-done.2
  89.5 0.0 copy-done.1
  89.5 0.0 copy-done
  89.5 0.2 conditional.1
  89.7 1.3 %copy.12 = bf16[128,8192]{1,0:T(8,128)(2,1)} copy(bf16[128,8192]{1,0:T(8,128)(2,1)S(1)} %get-tuple-element.32) | data formatting | bytes 4194304
Async XLA Ops:
  0.0 89.4 %copy-start.5 = (s32[4]{0:T(128)S(1)}, s32[4]{0:T(128)}, u32[]{:S(2)}) copy-start(s32[4]{0:T(128)} %own_ref.1) | copy-start | bytes 52
  0.0 89.4 %copy-start.4 = (s32[4]{0:T(128)S(1)}, s32[4]{0:T(128)}, u32[]{:S(2)}) copy-start(s32[4]{0:T(128)} %count_ref.1) | copy-start | bytes 52
  0.0 89.4 %copy-start.3 = (s32[4,8]{1,0:T(4,128)S(1)}, s32[4,8]{1,0:T(4,128)}, u32[]{:S(2)}) copy-start(s32[4,8]{1,0:T(4,128)} %sel_ref.1) | copy-start | bytes 388
  0.0 89.4 %copy-start.2 = (bf16[128,1024]{1,0:T(8,128)(2,1)S(1)}, bf16[128,1024]{1,0:T(8,128)(2,1)}, u32[]{:S(2)}) copy-start(bf16[128,1024]{1,0:T(8,128)(2,1)} %v_ref.1) | copy-start | bytes 786436
  0.0 89.4 %copy-start.1 = (bf16[128,1024]{1,0:T(8,128)(2,1)S(1)}, bf16[128,1024]{1,0:T(8,128)(2,1)}, u32[]{:S(2)}) copy-start(bf16[128,1024]{1,0:T(8,128)(2,1)} %k_ref.1) | copy-start | bytes 786436
  0.0 89.4 %copy-start = (bf16[128,8192]{1,0:T(8,128)(2,1)S(1)}, bf16[128,8192]{1,0:T(8,128)(2,1)}, u32[]{:S(2)}) copy-start(bf16[128,8192]{1,0:T(8,128)(2,1)} %q_ref.1) | copy-start | bytes 6291460
